TPU v7x, 32 devices: a whole 2x2x4 slice. The times are simulated.
32 devices in a mesh: elem: 8 (over z, core), lev: 4 (over y, x).
Axes of the slice: x: 2, y: 2, z: 4, core: 2. Of those that a mesh axis runs over, the one named last changes fastest.
Arguments:
- tracers: float32 [512, 16, 640], P('elem', 'lev'), may hold values from 0.1 to 120, as said below
- ref_index: int32 [512, 16], P('elem'), may hold values from 0 to 63
- requests: int32 [8, 2, 16], P('elem'), may hold values from -1 to 63, as said below
- source: int32 [512], P('elem'), may hold values from 0 to 95, as said below
- target_mean: float32 [40], replicated, may hold values from 0.5 to 5
Outputs:
- transported: float32 [512, 16, 640], P('elem', 'lev')
Inputs may be any that keep to these rules, and one draw needn't show every extreme that they name: Row 0 of requests[d] holds distinct element indices of block d - 1 (wrapping), row 1 of block d + 1; the valid entries come first and the rest are -1; every row holds 1 to 16 valid entries and some row holds exactly 16. `source`: every slot names an own element (below 64) or a valid entry of the block's requests: 64 + k for row 0, 80 + k for row 1. `tracers`: all entries are positive.
All inputs are finite; a program needn't handle non-finite values.
Results may differ from a plain program's by a relative error of at most 0.0003.
Values sent between devices are 32-bit elements; how exact they have to be, the bound alone decides.
No kernel may reach another device: no remote copies, remote signals or barrier semaphores. Data moves between devices by JAX's collectives and lax.ppermute only.
A program may use at most 64 MiB of HBM per device.

v0:
```python
import math

import jax
import jax.numpy as jnp
from jax import lax
from jax.sharding import PartitionSpec as P

NPTS = 16
REFS = 64


def with_halo(cells, sides, width):
    for axis, dim in sides:
        count = lax.axis_size(axis)
        head = lax.slice_in_dim(cells, 0, width, axis=dim)
        tail = lax.slice_in_dim(cells, cells.shape[dim] - width, cells.shape[dim], axis=dim)
        cells = jnp.concatenate(
            [
                lax.ppermute(tail, axis, [(i, (i + 1) % count) for i in range(count)]),
                cells,
                lax.ppermute(head, axis, [((i + 1) % count, i) for i in range(count)]),
            ],
            axis=dim,
        )
    return cells


def lagrange_table():
    side = math.isqrt(REFS)
    gll_nodes = [-1.0, -math.sqrt(0.2), math.sqrt(0.2), 1.0]
    points = -1.0 + 2.0 * jnp.arange(side, dtype=jnp.float32) / (side - 1)
    columns = []
    for which in range(4):
        basis = jnp.ones((side,), jnp.float32)
        for other in range(4):
            if other != which:
                basis = basis * (points - gll_nodes[other]) / (gll_nodes[which] - gll_nodes[other])
        columns.append(basis)
    one_dim = jnp.stack(columns, axis=1)
    return (one_dim[:, None, :, None] * one_dim[None, :, None, :]).reshape(side * side, 16)


def quadrature():
    edge = jnp.array([1.0 / 6.0, 5.0 / 6.0, 5.0 / 6.0, 1.0 / 6.0], jnp.float32)
    return (edge[:, None] * edge[None, :]).reshape(16)


def interpolate(source_rows, ref_index):
    elem_count, levels, width = source_rows.shape
    onehot = (ref_index[:, :, None] == jnp.arange(REFS, dtype=jnp.int32)[None, None, :]).astype(
        jnp.float32
    )
    matrix = jnp.einsum("epr,rn->epn", onehot, lagrange_table(), precision=lax.Precision.HIGHEST)
    values = source_rows.reshape(elem_count, levels * (width // 16), 16)
    result = jnp.einsum("epn,ecn->ecp", matrix, values, precision=lax.Precision.HIGHEST)
    lowest = jnp.min(values, axis=2, keepdims=True)
    highest = jnp.max(values, axis=2, keepdims=True)
    result = jnp.minimum(jnp.maximum(result, lowest), highest)
    return result.reshape(elem_count, levels, width)


def per_device(tracers, ref_index, requests, source, target_mean):
    elem_count, levels, width = tracers.shape
    beside_all = with_halo(tracers, (("elem", 0),), elem_count)
    own_pos = jnp.arange(elem_count, 2 * elem_count, dtype=jnp.int32)
    left_pos = jnp.maximum(requests[0, 0], 0)
    right_pos = 2 * elem_count + jnp.maximum(requests[0, 1], 0)
    slot_pos = jnp.concatenate([own_pos, left_pos, right_pos])
    source_rows = beside_all[slot_pos[source]]
    clipped = interpolate(source_rows, ref_index)
    tracer_count = width // NPTS
    shaped = clipped.reshape(elem_count, levels, tracer_count, NPTS)
    local_mass = jnp.einsum("eltn,n->t", shaped, quadrature(), precision=lax.Precision.HIGHEST)
    column_mass = lax.psum(local_mass, "lev")
    global_mass = lax.psum(column_mass, "elem")
    whole_weight = 4.0 * elem_count * lax.axis_size("elem") * levels * lax.axis_size("lev")
    factor = target_mean * whole_weight / global_mass
    return (shaped * factor[None, None, :, None]).reshape(elem_count, levels, width)


def solution(mesh):
    placed = (P("elem", "lev", None), P("elem", None), P("elem", None, None), P("elem"), P())
    return jax.shard_map(
        per_device, mesh=mesh, in_specs=placed, out_specs=P("elem", "lev", None), check_vma=False
    )
```

profile of v0, /device:TPU:0, one launch (start us, length us, event | category | flops | bytes accessed | tf_op | source)
XLA Modules:
  0.0 54.3 jit_solution(1006085163537011619)
XLA Ops:
  0.0 0.0 copy-start
  0.0 4.5 %collective-permute-start.1 = (f32[64,4,640]{2,1,0:T(4,128)}, f32[64,4,640]{2,1,0:T(4,128)S(1)}, u32[]{:S(2)}, u32[]{:S(2)}) collective-permute-start(f32[64,4,640]{2,1,0:T(4,128)} %param.6), channel_id=1, source_target_pairs={{4,0},{8,4},{12,8},{16,12},{20,16},{24,20},{28,24},{0,28},{5,1},{9... | collective-permute-start | bytes 1966088 | tf_op jit(solution)/shard_map/ppermute | solution.py:21
  4.5 0.0 collective-permute-start
  4.6 0.8 %maximum_bitcast_fusion = (s32[16]{0:T(128)S(1)}, s32[16]{0:T(128)S(1)}) fusion(s32[1,2,16]{2,1,0:T(2,128)} %param.8), kind=kLoop, calls=%fused_computation.29 | loop fusion | flops 48 | bytes 256 | tf_op jit(solution)/shard_map/max | solution.py:66
  5.3 0.1 broadcast_multiply_fusion
  5.4 0.1 reshape.146
  5.5 1.5 %fusion.1 = f32[64,16,16]{0,2,1:T(8,128)S(1)} fusion(f32[64,16,1]{0,1,2:T(8,128)S(1)} %reshape.146, s32[64,16]{0,1:T(8,128)} %param.7), kind=kOutput, calls=%fused_computation.8 | convolution fusion | flops 12648448 | bytes 73728 | tf_op jit(solution)/shard_map/epr,rn->epn/dot_general | solution.py:53
  7.0 1.0 %copy.23 = f32[64,16,16]{2,1,0:T(8,128)} copy(f32[64,16,16]{0,2,1:T(8,128)S(1)} %fusion.1) | data formatting | bytes 131072 | tf_op jit(solution)/shard_map/epr,rn->epn/dot_general | solution.py:53
  8.0 0.8 %broadcast_multiply_fusion.1 = f32[4,4]{1,0:T(4,128)S(1)} fusion(f32[4]{0:T(128)} %constant.76.clone), kind=kLoop, calls=%fused_computation.16 | loop fusion | flops 16 | bytes 80 | tf_op jit(solution)/shard_map/mul | solution.py:45
  8.8 0.1 reshape.147
  8.9 0.1 pad_add_fusion
  9.0 0.7 %compare_select_fusion.1 = s32[64]{0:T(128)S(1)} fusion(s32[64]{0:T(128)} %param.9), kind=kLoop, calls=%fused_computation.14 | loop fusion | flops 192 | bytes 512 | tf_op jit(solution)/shard_map/select_n | solution.py:69
  9.6 0.8 %gather_fusion = s32[64]{0:T(128)S(1)} fusion(s32[96]{0:T(128)S(1)} %pad_add_fusion, s32[1024]{0:T(1024)S(1)} %pad_clamp_fusion.1), kind=kCustom, calls=%fused_computation | custom fusion | bytes 768 | tf_op jit(solution)/shard_map/gather | solution.py:69
  10.4 7.6 %collective-permute-done.1 = f32[64,4,640]{2,1,0:T(4,128)S(1)} collective-permute-done((f32[64,4,640]{2,1,0:T(4,128)}, f32[64,4,640]{2,1,0:T(4,128)S(1)}, u32[]{:S(2)}, u32[]{:S(2)}) %collective-permute-start.1) | collective-permute-done | bytes 655392 | tf_op jit(solution)/shard_map/ppermute | solution.py:21
  18.0 3.0 %collective-permute-done = f32[64,4,640]{2,1,0:T(4,128)} collective-permute-done((f32[64,4,640]{2,1,0:T(4,128)}, f32[64,4,640]{2,1,0:T(4,128)}, u32[]{:S(2)}, u32[]{:S(2)}) %collective-permute-start) | collective-permute-done | bytes 655392 | tf_op jit(solution)/shard_map/ppermute | solution.py:19
  21.1 0.0 copy-done
  21.1 1.5 %pad_maximum_fusion = f32[192,4,640]{2,1,0:T(4,128)S(1)} fusion(f32[64,4,640]{2,1,0:T(4,128)S(1)} %collective-permute-done.1, f32[64,4,640]{2,1,0:T(4,128)S(1)} %copy-done, f32[64,4,640]{2,1,0:T(4,128)} %collective-permute-done), kind=kLoop, calls=%fused_computation.2 | loop fusion | flops 983040 | bytes 3932160 | tf_op jit(solution)/shard_map/concatenate | solution.py:17
  22.6 1.0 %gather_fusion.1 = f32[64,4,640]{2,1,0:T(4,128)S(1)} fusion(f32[192,4,640]{2,1,0:T(4,128)S(1)} %pad_maximum_fusion, s32[1024]{0:T(1024)S(1)} %pad_clamp_fusion), kind=kCustom, calls=%fused_computation.1 | custom fusion | bytes 1310976 | tf_op jit(solution)/shard_map/gather | solution.py:69
  23.5 0.4 copy.21
  24.0 0.5 fusion.7
  24.5 1.1 %copy.22 = f32[64,160,16]{1,2,0:T(8,128)S(1)} copy(f32[64,160,16]{0,2,1:T(8,128)S(1)} %bitcast.26) | data formatting | bytes 1310720 | tf_op jit(solution)/shard_map/reshape | solution.py:54
  25.6 0.0 copy-start.1
  25.6 0.1 copy.25
  25.7 0.1 copy.24
  25.8 2.1 %fusion.8 = (f32[160,16]{0,1:T(8,128)S(1)}, f32[64,160,16]{1,2,0:T(8,128)S(1)}) fusion(f32[64,160]{1,0:T(8,128)S(1)} %copy.25, f32[64,160]{1,0:T(8,128)S(1)} %copy.24, f32[64,160,16]{1,2,0:T(8,128)S(1)} %copy.22, f32[64,16,16]{2,1,0:T(8,128)} %copy.23), kind=kOutput, calls=%fused_computation.32 | convolution fusion | flops 31946240 | bytes 1468416 | tf_op jit(solution)/shard_map/epn,ecn->ecp/dot_general | solution.py:55
  28.0 0.1 reduce_sum.14
  28.1 0.1 convolution_bitcast_fusion
  28.2 9.9 %psum.14 = f32[40]{0:T(128)S(1)} all-reduce(f32[40]{0:T(128)S(1)} %convolution_bitcast_fusion), channel_id=1, replica_groups=mesh['elem'=8,'lev'=4] {'lev'}, use_global_device_ids=true, to_apply=%region_4.0 | all-reduce | flops 40 | bytes 320 | tf_op jit(solution)/shard_map/psum | solution.py:74
  38.1 13.6 %psum.15 = f32[40]{0:T(128)S(1)} all-reduce(f32[40]{0:T(128)S(1)} %psum.14), channel_id=1, replica_groups=mesh['elem'=8,'lev'=4] {'elem'}, use_global_device_ids=true, to_apply=%region_5.6 | all-reduce | flops 40 | bytes 320 | tf_op jit(solution)/shard_map/psum | solution.py:75
  51.7 0.0 copy-done.1
  51.7 0.1 mul.156
  51.8 0.1 mul.157
  51.8 1.1 %copy.26 = f32[64,160,16]{0,2,1:T(8,128)S(1)} copy(f32[64,160,16]{1,2,0:T(8,128)S(1)} %get-tuple-element.10) | data formatting | bytes 1310720 | tf_op jit(solution)/shard_map/min | solution.py:58
  52.9 0.2 bitcast_multiply_fusion
  53.1 1.2 %copy.27 = f32[64,4,640]{2,1,0:T(4,128)} copy(f32[64,4,640]{0,2,1:T(8,128)S(1)} %bitcast_multiply_fusion) | data formatting | bytes 1310720 | tf_op jit(solution)/shard_map/mul | solution.py:78
  (9 shorter events, 0.1 us)
Async XLA Ops:
  0.0 21.1 %copy-start = (f32[64,4,640]{2,1,0:T(4,128)S(1)}, f32[64,4,640]{2,1,0:T(4,128)}, u32[]{:S(2)}) copy-start(f32[64,4,640]{2,1,0:T(4,128)} %param.6) | copy-start | bytes 1966084
  0.0 18.0 %collective-permute-start.1 = (f32[64,4,640]{2,1,0:T(4,128)}, f32[64,4,640]{2,1,0:T(4,128)S(1)}, u32[]{:S(2)}, u32[]{:S(2)}) collective-permute-start(f32[64,4,640]{2,1,0:T(4,128)} %param.6), channel_id=1, source_target_pairs={{4,0},{8,4},{12,8},{16,12},{20,16},{24,20},{28,24},{0,28},{5,1},{9... | collective-permute-start | bytes 1966088 | tf_op jit(solution)/shard_map/ppermute | solution.py:21
  4.5 16.5 %collective-permute-start = (f32[64,4,640]{2,1,0:T(4,128)}, f32[64,4,640]{2,1,0:T(4,128)}, u32[]{:S(2)}, u32[]{:S(2)}) collective-permute-start(f32[64,4,640]{2,1,0:T(4,128)} %param.6), channel_id=1, source_target_pairs={{0,4},{4,8},{8,12},{12,16},{16,20},{20,24},{24,28},{28,0},{1,5},{5... | collective-permute-start | bytes 1966088 | tf_op jit(solution)/shard_map/ppermute | solution.py:19
  25.6 26.1 %copy-start.1 = (f32[40]{0:T(128)S(1)}, f32[40]{0:T(128)}, u32[]{:S(2)}) copy-start(f32[40]{0:T(128)} %param.10) | copy-start | bytes 484
where the time goes:
time: 54.6 us; the launch traced here: 54.3 us
  blocking collectives  23.5 us (43%)
  waiting for transfers between devices  10.6 us (19%)
  local copies, waits for them, and re-layouts  7.18 us (13%)
  other arithmetic  4.66 us (9%)
  starting transfers between devices  4.52 us (8%)
  matrix products  3.75 us (7%)
    psum x1, blocking collectives, per_device(): global_mass = lax.psum(column_mass, 'elem')  13.6 us
    psum x1, blocking collectives, per_device(): column_mass = lax.psum(local_mass, 'lev')  9.89 us
    ppermute x1, waiting for transfers between devices, with_halo(): lax.ppermute(head, axis, [((i + 1) % count, i) for i in range(count)])  7.59 us
    ppermute x1, starting transfers between devices, with_halo(): lax.ppermute(head, axis, [((i + 1) % count, i) for i in range(count)])  4.52 us
    ppermute x1, waiting for transfers between devices, with_halo(): lax.ppermute(tail, axis, [(i, (i + 1) % count) for i in range(count)])  3.03 us
    gather x3, local copies, waits for them, and re-layouts, per_device(): source_rows = beside_all[slot_pos[source]]  2.17 us
    dot_general x1, matrix products, interpolate(): jnp.einsum('epn,ecn->ecp', matrix, values, precision=lax.Precision.HIGHEST)  2.15 us
    concatenate x1, other arithmetic, with_halo(): jnp.concatenate([lax.ppermute(tail, axis, [(i, (i + 1) % count) for i in...  1.51 us
  transfers between devices with their start and end apart: 2, of which 2 were waited for; matrix products, arithmetic and copies ran while one was open for 11% of the time, Pallas kernels for 0%

commit v1 on v0

v1 whole, which is shorter than its diff:
```python
import functools
import math

import jax
import jax.numpy as jnp
import numpy as np
from jax import lax
from jax.experimental import pallas as pl
from jax.experimental.pallas import tpu as pltpu
from jax.sharding import PartitionSpec as P

NPTS = 16
REFS = 64
LANES = 128
SUB = 8

VMEM = pltpu.VMEM
SMEM = pltpu.SMEM


def lagrange_1d():
    side = math.isqrt(REFS)
    nodes = [np.float32(v) for v in (-1.0, -math.sqrt(0.2), math.sqrt(0.2), 1.0)]
    points = (-1.0 + 2.0 * np.arange(side, dtype=np.float32) / np.float32(side - 1)).astype(np.float32)
    columns = []
    for which in range(4):
        basis = np.ones((side,), np.float32)
        for other in range(4):
            if other != which:
                basis = basis * (points - nodes[other]) / (nodes[which] - nodes[other])
        columns.append(basis)
    return np.stack(columns, axis=1)


SIDE = math.isqrt(REFS)
BASIS = lagrange_1d()
WEIGHT36 = [ci * cj for ci in (1, 5, 5, 1) for cj in (1, 5, 5, 1)]


def split3(x):
    a = x.astype(jnp.bfloat16)
    rest = x - a.astype(jnp.float32)
    b = rest.astype(jnp.bfloat16)
    c = (rest - b.astype(jnp.float32)).astype(jnp.bfloat16)
    return a, b, c


def onehot_dot(parts, onehot):
    return sum(jnp.dot(part, onehot, preferred_element_type=jnp.float32) for part in parts)


def mm_nt(a, b):
    return lax.dot_general(a, b, (((1,), (1,)), ((), ())), preferred_element_type=jnp.float32)


class Sizes:
    def __init__(self, elems, levels, width, slots):
        self.elems, self.levels, self.width, self.slots = elems, levels, width, slots
        self.tracers = width // NPTS
        self.per = LANES // elems
        self.nv = levels // self.per
        self.cols = levels * elems
        self.tiles = width // LANES
        self.tpt = LANES // NPTS
        self.halves = LANES // (levels * slots)
        self.part = width // self.halves


def plan_kernel(z, req_ref, ref_ref, src_ref, wown_ref, payl_ref, payr_ref, codes_ref, coef_ref):
    elems, slots, levels = z.elems, z.slots, z.levels
    src = src_ref[...]
    lane = lax.broadcasted_iota(jnp.int32, (1, LANES), 1)
    k_lane = lane % slots
    first = jnp.full((1, elems), -1, jnp.int32)
    second = first
    pat_l = jnp.zeros((1, LANES), jnp.int32)
    pat_r = pat_l
    for k in range(slots):
        left, right = req_ref[0, 0, k], req_ref[0, 1, k]
        first = jnp.where(src == elems + k, left, first)
        second = jnp.where(src == elems + slots + k, right, second)
        pat_l = jnp.where(k_lane == k, left, pat_l)
        pat_r = jnp.where(k_lane == k, right, pat_r)
    ref = ref_ref[...]
    row = lax.broadcasted_iota(jnp.int32, (REFS, elems), 0)
    counts = jnp.zeros((REFS, elems), jnp.float32)
    for p in range(NPTS):
        counts = counts + jnp.where(row == ref[p : p + 1, :], float(WEIGHT36[p]), 0.0)
    counts = counts.astype(jnp.bfloat16)
    srow = lax.broadcasted_iota(jnp.int32, (LANES, elems), 0) % elems

    def weights(which):
        return mm_nt(counts, (srow == which).astype(jnp.float32).astype(jnp.bfloat16))

    wown_ref[...] = weights(src)
    payl_ref[0:REFS, :] = weights(first)
    payl_ref[REFS : REFS + SUB, :] = jnp.broadcast_to(pat_l.astype(jnp.float32), (SUB, LANES))
    payr_ref[0:REFS, :] = weights(second)
    payr_ref[REFS : REFS + SUB, :] = jnp.broadcast_to(pat_r.astype(jnp.float32), (SUB, LANES))

    src2 = jnp.concatenate([src] * z.per, axis=1)
    sub_level = lane // elems
    for v in range(z.nv):
        level = sub_level + v * z.per
        at = slice(v * LANES, (v + 1) * LANES)
        codes_ref[0:1, at] = jnp.where(src2 < elems, level * elems + src2, -1)
        rel = src2 - elems
        side = jnp.where(rel >= slots, 1, 0)
        code = side * LANES + level * slots + (rel - side * slots)
        for h in range(z.halves):
            codes_ref[1 + h : 2 + h, at] = jnp.where(rel >= 0, code + h * levels * slots, -1)

    ref2 = jnp.concatenate([ref] * z.per, axis=1)
    one, two = ref2 // SIDE, ref2 % SIDE

    def basis(which):
        found = []
        for i in range(4):
            value = jnp.zeros(which.shape, jnp.float32)
            for a in range(SIDE):
                if BASIS[a, i] != 0.0:
                    value = jnp.where(which == a, float(BASIS[a, i]), value)
            found.append(value)
        return found

    la, lb = basis(one), basis(two)
    for i in range(4):
        for j in range(4):
            n = 4 * i + j
            coef_ref[n * NPTS : (n + 1) * NPTS, :] = la[i] * lb[j]


def line(x):
    out = [None] * SIDE
    out[0], out[SIDE - 1] = x[0], x[3]
    outer, inner = x[0] + x[3], x[1] + x[2]
    outer_odd, inner_odd = x[0] - x[3], x[1] - x[2]
    for a in range(1, SIDE // 2):
        c = [float(v) for v in BASIS[a]]
        even = (0.5 * (c[0] + c[3])) * outer + (0.5 * (c[1] + c[2])) * inner
        odd = (0.5 * (c[0] - c[3])) * outer_odd + (0.5 * (c[1] - c[2])) * inner_odd
        out[a], out[SIDE - 1 - a] = even + odd, even - odd
    return out


def tree(op, values):
    while len(values) > 1:
        values = [op(values[i], values[i + 1]) if i + 1 < len(values) else values[i] for i in range(0, len(values), 2)]
    return values[0]


def prep_kernel(z, x_ref, codes_ref, xt_ref, parts_ref, own_ref, sums_ref):
    step = z.tiles * z.levels
    for j in range(z.tiles):
        for v in range(z.nv):
            rows = []
            for q in range(z.per):
                level = v * z.per + q
                for e in range(0, z.elems, SUB):
                    rows.append(x_ref[pl.ds(e * step + j * z.levels + level, SUB, stride=step), :])
            block = jnp.concatenate(rows, axis=0)
            xt_ref[v, j * LANES : (j + 1) * LANES, :] = block.T
    a, b, c = split3(jnp.concatenate([xt_ref[v] for v in range(z.nv)], axis=1))
    parts_ref[0], parts_ref[1], parts_ref[2] = a, b, c
    row = lax.broadcasted_iota(jnp.int32, (z.cols, z.cols), 0)
    pick = (row == codes_ref[0:1, :]).astype(jnp.float32).astype(jnp.bfloat16)
    own_ref[...] = onehot_dot((a, b, c), pick)
    for j in range(z.tiles):
        both = [None] * REFS
        for v in range(z.nv):
            x = [xt_ref[v, pl.ds(j * LANES + n, z.tpt, stride=NPTS), :] for n in range(NPTS)]
            lowest, highest = tree(jnp.minimum, x), tree(jnp.maximum, x)
            lines = [line(x[4 * i : 4 * i + 4]) for i in range(4)]
            for b in range(SIDE):
                column = line([lines[i][b] for i in range(4)])
                for a in range(SIDE):
                    value = jnp.minimum(jnp.maximum(column[a], lowest), highest)
                    r = a * SIDE + b
                    both[r] = value if both[r] is None else both[r] + value
        for r in range(REFS):
            sums_ref[r * z.tracers + j * z.tpt : r * z.tracers + (j + 1) * z.tpt, :] = both[r]


def serve_kernel(z, wown_ref, inl_ref, inr_ref, sums_ref, parts_ref, mass_ref, tol_ref, tor_ref, weight_ref):
    weight_ref[...] = wown_ref[...] + inl_ref[0:REFS, :] + inr_ref[0:REFS, :]
    lane = lax.broadcasted_iota(jnp.int32, (1, LANES), 1)
    level = (lane // z.slots) % z.levels
    codes = []
    for ref in (inl_ref, inr_ref):
        wanted = ref[REFS : REFS + 1, :].astype(jnp.int32)
        codes.append(jnp.where(wanted >= 0, level * z.elems + wanted, -1))
    code = jnp.concatenate(codes, axis=1)
    row = lax.broadcasted_iota(jnp.int32, (z.cols, 2 * LANES), 0)
    pick = (row == code).astype(jnp.float32).astype(jnp.bfloat16)
    rows = onehot_dot((parts_ref[0], parts_ref[1], parts_ref[2]), pick)
    half = lane // (z.levels * z.slots)
    for ref, at in ((tor_ref, slice(0, LANES)), (tol_ref, slice(LANES, 2 * LANES))):
        value = rows[0 : z.part, at]
        for h in range(1, z.halves):
            value = jnp.where(half == h, rows[h * z.part : (h + 1) * z.part, at], value)
        ref[...] = value
    total = [None] * z.tiles
    for r in range(REFS):
        w = weight_ref[pl.ds(r, 1), :]
        for j in range(z.tiles):
            lo = r * z.tracers + j * z.tpt
            term = sums_ref[lo : lo + z.tpt, :] * w
            total[j] = term if total[j] is None else total[j] + term
    total = jnp.concatenate(total, axis=0)
    ones = jnp.ones((SUB, LANES), jnp.bfloat16)
    parts = split3(total)
    mass_ref[...] = sum(mm_nt(ones, part) for part in parts)[0:1, :]


def final_kernel(z, own_ref, froml_ref, fromr_ref, codes_ref, coef_ref, out_ref, got_ref, turn_ref):
    halo = jnp.concatenate([froml_ref[...], fromr_ref[...]], axis=1)
    parts = split3(halo)
    row = lax.broadcasted_iota(jnp.int32, (2 * LANES, z.cols), 0)
    for h in range(z.halves):
        pick = (row == codes_ref[1 + h : 2 + h, :]).astype(jnp.float32).astype(jnp.bfloat16)
        at = slice(h * z.part, (h + 1) * z.part)
        got = own_ref[at, :] + onehot_dot(parts, pick)
        for v in range(z.nv):
            got_ref[v, at, :] = got[:, v * LANES : (v + 1) * LANES]
    step = z.tiles * z.levels
    for j in range(z.tiles):
        xs, low, high = [], [], []
        for v in range(z.nv):
            x = [got_ref[v, pl.ds(j * LANES + n, z.tpt, stride=NPTS), :] for n in range(NPTS)]
            xs.append(x)
            low.append(tree(jnp.minimum, x))
            high.append(tree(jnp.maximum, x))
        for p in range(NPTS):
            coef = [coef_ref[pl.ds(n * NPTS + p, 1), :] for n in range(NPTS)]
            for v in range(z.nv):
                value = tree(jnp.add, [coef[n] * xs[v][n] for n in range(NPTS)])
                value = jnp.minimum(jnp.maximum(value, low[v]), high[v])
                turn_ref[v, pl.ds(p, z.tpt, stride=NPTS), :] = value
        for v in range(z.nv):
            block = turn_ref[v].T
            for q in range(z.per):
                level = v * z.per + q
                for e in range(0, z.elems, SUB):
                    piece = block[q * z.elems + e : q * z.elems + e + SUB, :]
                    out_ref[pl.ds(e * step + j * z.levels + level, SUB, stride=step), :] = piece


def call(kernel, z, name, outs, ins, args, scratch=(), flops=0, nbytes=0):
    return pl.pallas_call(
        functools.partial(kernel, z),
        out_shape=[jax.ShapeDtypeStruct(shape, dtype) for shape, dtype in outs],
        in_specs=[pl.BlockSpec(memory_space=space) for space in ins],
        out_specs=[pl.BlockSpec(memory_space=VMEM)] * len(outs),
        scratch_shapes=list(scratch),
        cost_estimate=pl.CostEstimate(flops=flops, bytes_accessed=nbytes, transcendentals=0),
        name=name,
    )(*args)


def per_device(tracers, ref_index, requests, source, target_mean):
    elems, levels, width = tracers.shape
    z = Sizes(elems, levels, width, requests.shape[2])
    assert z.per * elems == LANES and z.nv * z.per == levels and z.tiles * LANES == width
    assert z.halves * levels * z.slots == LANES and z.part * z.halves == width
    f32, bf16, i32 = jnp.float32, jnp.bfloat16, jnp.int32
    flat = tracers.reshape(elems, levels, z.tiles, LANES).transpose(0, 2, 1, 3).reshape(-1, LANES)

    wown, payl, payr, codes, coef = call(
        plan_kernel, z, "plan",
        [((REFS, LANES), f32), ((REFS + SUB, LANES), f32), ((REFS + SUB, LANES), f32), ((SUB, z.cols), i32),
         ((NPTS * NPTS, LANES), f32)],
        (SMEM, VMEM, VMEM), (requests, ref_index.T, source.reshape(1, elems)), flops=10**6, nbytes=10**5,
    )
    count = lax.axis_size("elem")
    to_right = [(i, (i + 1) % count) for i in range(count)]
    to_left = [((i + 1) % count, i) for i in range(count)]
    inl = lax.ppermute(payl, "elem", to_left)
    inr = lax.ppermute(payr, "elem", to_right)
    _, parts, own, sums = call(
        prep_kernel, z, "prep",
        [((z.nv, width, LANES), f32), ((3, width, z.cols), bf16), ((width, z.cols), f32), ((REFS * z.tracers, LANES), f32)],
        (VMEM, VMEM), (flat, codes), flops=10**8, nbytes=4 * 10**6,
    )
    mass, tol, tor = call(
        serve_kernel, z, "serve",
        [((1, z.tracers), f32), ((z.part, LANES), f32), ((z.part, LANES), f32)],
        (VMEM,) * 5, (wown, inl, inr, sums, parts), [VMEM((REFS, LANES), f32)], flops=10**7, nbytes=3 * 10**6,
    )
    froml = lax.ppermute(tor, "elem", to_right)
    fromr = lax.ppermute(tol, "elem", to_left)
    axes = ("elem", "lev")
    members = lax.axis_size(axes)
    spread = jnp.broadcast_to(mass[None], (members, 1, z.tracers))
    every = lax.all_to_all(spread, axes, 0, 0)
    (shaped,) = call(
        final_kernel, z, "final",
        [((elems * levels * z.tiles, LANES), f32)],
        (VMEM,) * 5, (own, froml, fromr, codes, coef),
        [VMEM((z.nv, width, LANES), f32), VMEM((z.nv, LANES, LANES), f32)], flops=10**8, nbytes=3 * 10**6,
    )
    shaped = shaped.reshape(elems, z.tiles, levels, LANES).transpose(0, 2, 1, 3).reshape(elems, levels, width)
    global_mass = every.sum(axis=(0, 1))
    whole_weight = 36.0 * 4.0 * elems * count * levels * lax.axis_size("lev")
    factor = target_mean * whole_weight / global_mass
    return shaped * jnp.repeat(factor, NPTS)[None, None, :]


def solution(mesh):
    placed = (P("elem", "lev", None), P("elem", None), P("elem", None, None), P("elem"), P())
    return jax.shard_map(
        per_device, mesh=mesh, in_specs=placed, out_specs=P("elem", "lev", None), check_vma=False
    )
```

time: 54.6 us -> 38.4 us (0.70)
  blocking collectives: 23.5 us -> 0 us
  Pallas kernels: 0 us -> 12 us
  starting transfers between devices: 4.52 us -> 13.9 us
  waiting for transfers between devices: 10.6 us -> 3.73 us
  other arithmetic: 4.66 us -> 0.07 us
  matrix products: 3.75 us -> 0 us
  local copies, waits for them, and re-layouts: 7.18 us -> 7.84 us
    psum x2 -> x0, blocking collectives: 23.5 us -> none  [the longest x1 13.6 us: per_device(): global_mass = lax.psum(column_mass, 'elem')]
    pallas_call x0 -> x4, Pallas kernels: none -> 12 us  [call(): pl.pallas_call(functools.partial(kernel, z), out_shape=[jax.ShapeDtypeStr...]
    ppermute x2 -> x4, waiting for transfers between devices: 10.6 us -> 0.01 us  [the longest x1 0.01 us: per_device(): inr = lax.ppermute(payr, 'elem', to_right)]
    all_to_all x0 -> x1, starting transfers between devices: none -> 5.79 us  [per_device(): every = lax.all_to_all(spread, axes, 0, 0)]
    dot_general x3 -> x0, matrix products: 3.75 us -> none  [the longest x1 2.15 us: interpolate(): jnp.einsum('epn,ecn->ecp', matrix, values, precision=lax.Precision.HIGHEST)]
    all_to_all x0 -> x1, waiting for transfers between devices: none -> 3.72 us  [per_device(): every = lax.all_to_all(spread, axes, 0, 0)]
    ppermute x2 -> x4, starting transfers between devices: 4.52 us -> 8.12 us  [the longest x1 4.52 us: per_device(): inl = lax.ppermute(payl, 'elem', to_left)]
    unnamed x4 -> x11, local copies, waits for them, and re-layouts: 0.01 us -> 2.44 us
  transfers between devices with their start and end apart: 2 -> 5, of which waited for: 2 -> 1; matrix products, arithmetic and copies ran while one was open for 11% -> 7% of each run, Pallas kernels for 0% -> 10%
where the time goes in v1:
time: 38.4 us; the launch traced here: 37.7 us
  starting transfers between devices  13.9 us (36%)
  Pallas kernels  12 us (31%)
  local copies, waits for them, and re-layouts  7.84 us (20%)
  waiting for transfers between devices  3.73 us (10%)
    pallas_call x4, Pallas kernels, call(): pl.pallas_call(functools.partial(kernel, z), out_shape=[jax.ShapeDtypeStr...  12 us
    all_to_all x1, starting transfers between devices, per_device(): every = lax.all_to_all(spread, axes, 0, 0)  5.79 us
    ppermute x1, starting transfers between devices, per_device(): inl = lax.ppermute(payl, 'elem', to_left)  4.52 us
    all_to_all x1, waiting for transfers between devices, per_device(): every = lax.all_to_all(spread, axes, 0, 0)  3.72 us
    ppermute x1, starting transfers between devices, per_device(): fromr = lax.ppermute(tol, 'elem', to_left)  3.29 us
    unnamed x11, local copies, waits for them, and re-layouts  2.44 us
    reshape x2, local copies, waits for them, and re-layouts, per_device(): shaped.reshape(elems, z.tiles, levels, LANES).transpose(0, 2, 1, 3)  1.4 us
    mul x2, local copies, waits for them, and re-layouts, per_device(): return shaped * jnp.repeat(factor, NPTS)[None, None, :]  1.34 us
  transfers between devices with their start and end apart: 5, of which 1 were waited for; matrix products, arithmetic and copies ran while one was open for 7% of the time, Pallas kernels for 10%

profile of v1, /device:TPU:0, one launch (start us, length us, event | category | flops | bytes accessed | tf_op | source)
XLA Modules:
  0.0 37.7 jit_solution(4476509843034739891)
XLA Ops:
  0.0 1.6 %plan.1 = (f32[64,128]{1,0:T(8,128)}, f32[72,128]{1,0:T(8,128)}, f32[72,128]{1,0:T(8,128)}, s32[8,256]{1,0:T(8,128)}, f32[256,128]{1,0:T(8,128)}) custom-call(s32[1,2,16]{2,1,0:T(2,128)} %req_ref.1, s32[16,64]{1,0:T(8,128)} %bitcast.19, s32[1,64]{1,0:T(1,128)} %bitcast.20), custom_call_target="tpu_custom_call" | custom-call | flops 1000000 | bytes 100000 | tf_op jit(solution)/shard_map/plan/pallas_call | solution.py:249
  1.6 4.5 %collective-permute-start = (f32[72,128]{1,0:T(8,128)}, f32[72,128]{1,0:T(8,128)S(1)}, u32[]{:S(2)}, u32[]{:S(2)}) collective-permute-start(f32[72,128]{1,0:T(8,128)} %get-tuple-element.19), channel_id=1, source_target_pairs={{4,0},{8,4},{12,8},{16,12},{20,16},{24,20},{28,24},{0,28},{5,1},{9... | collective-permute-start | bytes 110600 | tf_op jit(solution)/shard_map/ppermute | solution.py:277
  6.1 0.0 collective-permute-start.1
  6.1 1.1 %copy.16 = f32[64,4,640]{2,0,1:T(8,128)S(1)} copy(f32[64,4,640]{2,1,0:T(4,128)} %param.5) | data formatting | bytes 1310720 | tf_op args[0]
  7.2 0.1 reshape.19
  7.3 1.3 %copy.17 = f32[64,5,4,128]{3,2,1,0:T(4,128)} copy(f32[64,5,4,128]{3,1,0,2:T(8,128)S(1)} %bitcast.14) | data formatting | bytes 1310720 | tf_op jit(solution)/shard_map/transpose | solution.py:266
  8.6 3.9 %prep.1 = (f32[2,640,128]{2,1,0:T(8,128)}, bf16[3,640,256]{2,1,0:T(8,128)(2,1)}, f32[640,256]{1,0:T(8,128)}, f32[2560,128]{1,0:T(8,128)}) custom-call(f32[1280,128]{1,0:T(8,128)} %bitcast.17, s32[8,256]{1,0:T(8,128)} %get-tuple-element.16.codes_ref), custom_call_target="tpu_custom_call" | custom-call | flops 100000000 | bytes 4000000 | tf_op jit(solution)/shard_map/prep/pallas_call | solution.py:249
  12.5 0.0 copy-start.4
  12.5 0.0 collective-permute-done.inl_ref
  12.5 0.0 copy-start.2
  12.5 0.0 collective-permute-done.1.inr_ref
  12.5 0.0 copy-start.3
  12.6 0.6 %copy-done.2 = f32[72,128]{1,0:T(8,128)} copy-done((f32[72,128]{1,0:T(8,128)}, f32[72,128]{1,0:T(8,128)S(1)}, u32[]{:S(2)}) %copy-start.2) | copy-done | bytes 36888
  13.1 0.0 copy-done.3
  13.2 2.8 %serve.1 = (f32[1,40]{1,0:T(1,128)}, f32[320,128]{1,0:T(8,128)}, f32[320,128]{1,0:T(8,128)}) custom-call(f32[64,128]{1,0:T(8,128)} %get-tuple-element.18.wown_ref, f32[72,128]{1,0:T(8,128)} %copy-done.2, f32[72,128]{1,0:T(8,128)} %copy-done.3, f32[2560,128]{1,0:T(8,128)} %get-tuple-element.21.sums_ref, bf16[3,640,256]{2,1,0:T(8,128)(2,1)} %get-tuple-element.22.parts_ref), custom_call_target="tpu_custom_call" | custom-call | flops 10000000 | bytes 3000000 | tf_op jit(solution)/shard_map/serve/pallas_call | solution.py:249
  16.0 1.2 %broadcast_in_dim.12 = f32[32,1,40]{2,1,0:T(1,128)} broadcast(f32[40]{0:T(128)} %bitcast.21), dimensions={2} | broadcast | bytes 5280 | tf_op jit(solution)/shard_map/broadcast_in_dim | solution.py:293
  17.2 5.8 %all-to-all-start = ((f32[32,1,40]{2,1,0:T(1,128)}), f32[32,1,40]{2,1,0:T(1,128)S(1)}, u32[]{:S(2)}, u32[]{:S(2)}) async-start(f32[32,1,40]{2,1,0:T(1,128)} %broadcast_in_dim.12), calls=%async_computation | async-start | bytes 32768 | tf_op jit(solution)/shard_map/all_to_all | solution.py:294
  23.0 0.3 collective-permute-start.2
  23.3 3.3 %collective-permute-start.3 = (f32[320,128]{1,0:T(8,128)}, f32[320,128]{1,0:T(8,128)S(1)}, u32[]{:S(2)}, u32[]{:S(2)}) collective-permute-start(f32[320,128]{1,0:T(8,128)} %get-tuple-element.24), channel_id=1, source_target_pairs={{4,0},{8,4},{12,8},{16,12},{20,16},{24,20},{28,24},{0,28},{5,1},{9... | collective-permute-start | bytes 491528 | tf_op jit(solution)/shard_map/ppermute | solution.py:290
  26.6 3.7 %all-to-all-done = f32[32,1,40]{2,1,0:T(1,128)S(1)} async-done(((f32[32,1,40]{2,1,0:T(1,128)}), f32[32,1,40]{2,1,0:T(1,128)S(1)}, u32[]{:S(2)}, u32[]{:S(2)}) %all-to-all-start) | async-done | bytes 5152 | tf_op jit(solution)/shard_map/all_to_all | solution.py:294
  30.4 0.0 copy-done.4
  30.4 0.1 broadcast_in_dim.13
  30.4 0.1 mul.18
  30.5 0.0 collective-permute-done.2.froml_ref
  30.5 0.0 copy-start
  30.5 0.0 collective-permute-done.3.fromr_ref
  30.5 0.0 copy-start.1
  30.6 0.6 %copy-done = f32[320,128]{1,0:T(8,128)} copy-done((f32[320,128]{1,0:T(8,128)}, f32[320,128]{1,0:T(8,128)S(1)}, u32[]{:S(2)}) %copy-start) | copy-done | bytes 163864
  31.2 0.1 copy-done.1
  31.3 3.7 %final.1 = f32[1280,128]{1,0:T(8,128)} custom-call(f32[640,256]{1,0:T(8,128)} %get-tuple-element.17.own_ref, f32[320,128]{1,0:T(8,128)} %copy-done, f32[320,128]{1,0:T(8,128)} %copy-done.1, s32[8,256]{1,0:T(8,128)} %get-tuple-element.16.codes_ref, f32[256,128]{1,0:T(8,128)} %get-tuple-element.25.coef_ref), custom_call_target="tpu_custom_call" | custom-call | flops 100000000 | bytes 3000000 | tf_op jit(solution)/shard_map/final/pallas_call | solution.py:249
  34.9 1.2 %copy.22 = f32[64,5,4,128]{3,1,0,2:T(8,128)S(1)} copy(f32[64,5,4,128]{3,2,1,0:T(4,128)} %bitcast.16) | data formatting | bytes 1310720 | tf_op jit(solution)/shard_map/reshape | solution.py:301
  36.2 0.2 reshape.23
  36.4 1.3 %copy.20 = f32[64,4,640]{2,1,0:T(4,128)} copy(f32[64,4,640]{2,0,1:T(8,128)S(1)} %broadcast_multiply_fusion) | data formatting | bytes 1310720 | tf_op jit(solution)/shard_map/mul | solution.py:305
  (3 shorter events, 0.1 us)
Async XLA Ops:
  1.6 11.0 %collective-permute-start = (f32[72,128]{1,0:T(8,128)}, f32[72,128]{1,0:T(8,128)S(1)}, u32[]{:S(2)}, u32[]{:S(2)}) collective-permute-start(f32[72,128]{1,0:T(8,128)} %get-tuple-element.19), channel_id=1, source_target_pairs={{4,0},{8,4},{12,8},{16,12},{20,16},{24,20},{28,24},{0,28},{5,1},{9... | collective-permute-start | bytes 110600 | tf_op jit(solution)/shard_map/ppermute | solution.py:277
  6.1 6.5 %collective-permute-start.1 = (f32[72,128]{1,0:T(8,128)}, f32[72,128]{1,0:T(8,128)S(1)}, u32[]{:S(2)}, u32[]{:S(2)}) collective-permute-start(f32[72,128]{1,0:T(8,128)} %get-tuple-element.20), channel_id=1, source_target_pairs={{0,4},{4,8},{8,12},{12,16},{16,20},{20,24},{24,28},{28,0},{1,5},{5... | collective-permute-start | bytes 110600 | tf_op jit(solution)/shard_map/ppermute | solution.py:278
  12.5 17.8 %copy-start.4 = (f32[40]{0:T(128)S(1)}, f32[40]{0:T(128)}, u32[]{:S(2)}) copy-start(f32[40]{0:T(128)} %param.9) | copy-start | bytes 484
  12.5 0.6 %copy-start.2 = (f32[72,128]{1,0:T(8,128)}, f32[72,128]{1,0:T(8,128)S(1)}, u32[]{:S(2)}) copy-start(f32[72,128]{1,0:T(8,128)S(1)} %collective-permute-done.inl_ref) | copy-start | bytes 110596
  12.5 0.6 %copy-start.3 = (f32[72,128]{1,0:T(8,128)}, f32[72,128]{1,0:T(8,128)S(1)}, u32[]{:S(2)}) copy-start(f32[72,128]{1,0:T(8,128)S(1)} %collective-permute-done.1.inr_ref) | copy-start | bytes 110596
  17.2 13.1 %all-to-all-start = ((f32[32,1,40]{2,1,0:T(1,128)}), f32[32,1,40]{2,1,0:T(1,128)S(1)}, u32[]{:S(2)}, u32[]{:S(2)}) async-start(f32[32,1,40]{2,1,0:T(1,128)} %broadcast_in_dim.12), calls=%async_computation | async-start | bytes 32768 | tf_op jit(solution)/shard_map/all_to_all | solution.py:294
  23.0 7.5 %collective-permute-start.2 = (f32[320,128]{1,0:T(8,128)}, f32[320,128]{1,0:T(8,128)S(1)}, u32[]{:S(2)}, u32[]{:S(2)}) collective-permute-start(f32[320,128]{1,0:T(8,128)} %get-tuple-element.23), channel_id=1, source_target_pairs={{0,4},{4,8},{8,12},{12,16},{16,20},{20,24},{24,28},{28,0},{1,5},{5... | collective-permute-start | bytes 491528 | tf_op jit(solution)/shard_map/ppermute | solution.py:289
  23.3 7.2 %collective-permute-start.3 = (f32[320,128]{1,0:T(8,128)}, f32[320,128]{1,0:T(8,128)S(1)}, u32[]{:S(2)}, u32[]{:S(2)}) collective-permute-start(f32[320,128]{1,0:T(8,128)} %get-tuple-element.24), channel_id=1, source_target_pairs={{4,0},{8,4},{12,8},{16,12},{20,16},{24,20},{28,24},{0,28},{5,1},{9... | collective-permute-start | bytes 491528 | tf_op jit(solution)/shard_map/ppermute | solution.py:290
  30.5 0.7 %copy-start = (f32[320,128]{1,0:T(8,128)}, f32[320,128]{1,0:T(8,128)S(1)}, u32[]{:S(2)}) copy-start(f32[320,128]{1,0:T(8,128)S(1)} %collective-permute-done.2.froml_ref) | copy-start | bytes 491524
  30.5 0.7 %copy-start.1 = (f32[320,128]{1,0:T(8,128)}, f32[320,128]{1,0:T(8,128)S(1)}, u32[]{:S(2)}) copy-start(f32[320,128]{1,0:T(8,128)S(1)} %collective-permute-done.3.fromr_ref) | copy-start | bytes 491524

commit v2 on v1

--- a/solution.py
+++ b/solution.py
@@ -8,6 +8,7 @@
 from jax.experimental import pallas as pl
 from jax.experimental.pallas import tpu as pltpu
 from jax.sharding import PartitionSpec as P
+
 
 NPTS = 16
 REFS = 64
@@ -66,8 +67,24 @@
         self.part = width // self.halves
 
 
-def plan_kernel(z, req_ref, ref_ref, src_ref, wown_ref, payl_ref, payr_ref, codes_ref, coef_ref):
-    elems, slots, levels = z.elems, z.slots, z.levels
+def plan_kernel(
+    z, x_hbm, req_hbm, ref_hbm, src_hbm, wown_ref, payl_ref, payr_ref, raw_ref, ref_ref, src_ref, req_ref, sem, xsem
+):
+    elems, slots = z.elems, z.slots
+    small = [
+        pltpu.make_async_copy(src, dst, sem.at[i])
+        for i, (src, dst) in enumerate(((req_hbm, req_ref), (ref_hbm, ref_ref), (src_hbm, src_ref)))
+    ]
+    large = [
+        pltpu.make_async_copy(
+            x_hbm.at[:, :, pl.ds(j * LANES, LANES)], raw_ref.at[j].reshape(elems, z.levels, LANES), xsem.at[j]
+        )
+        for j in range(z.tiles)
+    ]
+    for copy in small + large:
+        copy.start()
+    for copy in small:
+        copy.wait()
     src = src_ref[...]
     lane = lax.broadcasted_iota(jnp.int32, (1, LANES), 1)
     k_lane = lane % slots
@@ -97,7 +114,13 @@
     payl_ref[REFS : REFS + SUB, :] = jnp.broadcast_to(pat_l.astype(jnp.float32), (SUB, LANES))
     payr_ref[0:REFS, :] = weights(second)
     payr_ref[REFS : REFS + SUB, :] = jnp.broadcast_to(pat_r.astype(jnp.float32), (SUB, LANES))
-
+    for copy in large:
+        copy.wait()
+
+
+def tables(z, src, ref, codes_ref, coef_ref):
+    elems, slots, levels = z.elems, z.slots, z.levels
+    lane = lax.broadcasted_iota(jnp.int32, (1, LANES), 1)
     src2 = jnp.concatenate([src] * z.per, axis=1)
     sub_level = lane // elems
     for v in range(z.nv):
@@ -149,15 +172,15 @@
     return values[0]
 
 
-def prep_kernel(z, x_ref, codes_ref, xt_ref, parts_ref, own_ref, sums_ref):
-    step = z.tiles * z.levels
+def prep_kernel(z, raw_ref, ref_ref, src_ref, parts_ref, own_ref, sums_ref, codes_ref, coef_ref, xt_ref):
+    tables(z, src_ref[...], ref_ref[...], codes_ref, coef_ref)
     for j in range(z.tiles):
         for v in range(z.nv):
             rows = []
             for q in range(z.per):
                 level = v * z.per + q
                 for e in range(0, z.elems, SUB):
-                    rows.append(x_ref[pl.ds(e * step + j * z.levels + level, SUB, stride=step), :])
+                    rows.append(raw_ref[j, pl.ds(e * z.levels + level, SUB, stride=z.levels), :])
             block = jnp.concatenate(rows, axis=0)
             xt_ref[v, j * LANES : (j + 1) * LANES, :] = block.T
     a, b, c = split3(jnp.concatenate([xt_ref[v] for v in range(z.nv)], axis=1))
@@ -212,7 +235,7 @@
     mass_ref[...] = sum(mm_nt(ones, part) for part in parts)[0:1, :]
 
 
-def final_kernel(z, own_ref, froml_ref, fromr_ref, codes_ref, coef_ref, out_ref, got_ref, turn_ref):
+def final_kernel(z, own_ref, froml_ref, fromr_ref, codes_ref, coef_ref, out_ref, got_ref, turn_ref, flat_ref, sem):
     halo = jnp.concatenate([froml_ref[...], fromr_ref[...]], axis=1)
     parts = split3(halo)
     row = lax.broadcasted_iota(jnp.int32, (2 * LANES, z.cols), 0)
@@ -222,7 +245,7 @@
         got = own_ref[at, :] + onehot_dot(parts, pick)
         for v in range(z.nv):
             got_ref[v, at, :] = got[:, v * LANES : (v + 1) * LANES]
-    step = z.tiles * z.levels
+    copies = []
     for j in range(z.tiles):
         xs, low, high = [], [], []
         for v in range(z.nv):
@@ -242,10 +265,22 @@
                 level = v * z.per + q
                 for e in range(0, z.elems, SUB):
                     piece = block[q * z.elems + e : q * z.elems + e + SUB, :]
-                    out_ref[pl.ds(e * step + j * z.levels + level, SUB, stride=step), :] = piece
-
-
-def call(kernel, z, name, outs, ins, args, scratch=(), flops=0, nbytes=0):
+                    flat_ref[j, pl.ds(e * z.levels + level, SUB, stride=z.levels), :] = piece
+        copies.append(
+            pltpu.make_async_copy(
+                flat_ref.at[j].reshape(z.elems, z.levels, LANES), out_ref.at[:, :, pl.ds(j * LANES, LANES)], sem.at[j]
+            )
+        )
+        copies[-1].start()
+    for copy in copies:
+        copy.wait()
+
+
+def in_hbm(x):
+    return pltpu.with_memory_space_constraint(x, pltpu.HBM)
+
+
+def call(kernel, z, outs, ins, args, scratch=(), flops=0, nbytes=0, limit=16):
     return pl.pallas_call(
         functools.partial(kernel, z),
         out_shape=[jax.ShapeDtypeStruct(shape, dtype) for shape, dtype in outs],
@@ -253,7 +288,7 @@
         out_specs=[pl.BlockSpec(memory_space=VMEM)] * len(outs),
         scratch_shapes=list(scratch),
         cost_estimate=pl.CostEstimate(flops=flops, bytes_accessed=nbytes, transcendentals=0),
-        name=name,
+        compiler_params=pltpu.CompilerParams(vmem_limit_bytes=limit << 20),
     )(*args)
 
 
@@ -263,26 +298,28 @@
     assert z.per * elems == LANES and z.nv * z.per == levels and z.tiles * LANES == width
     assert z.halves * levels * z.slots == LANES and z.part * z.halves == width
     f32, bf16, i32 = jnp.float32, jnp.bfloat16, jnp.int32
-    flat = tracers.reshape(elems, levels, z.tiles, LANES).transpose(0, 2, 1, 3).reshape(-1, LANES)
-
-    wown, payl, payr, codes, coef = call(
-        plan_kernel, z, "plan",
-        [((REFS, LANES), f32), ((REFS + SUB, LANES), f32), ((REFS + SUB, LANES), f32), ((SUB, z.cols), i32),
-         ((NPTS * NPTS, LANES), f32)],
-        (SMEM, VMEM, VMEM), (requests, ref_index.T, source.reshape(1, elems)), flops=10**6, nbytes=10**5,
+    flat = ((z.tiles, elems * levels, LANES), f32)
+    wown, payl, payr, raw, refs, own_source = call(
+        plan_kernel, z,
+        [((REFS, LANES), f32), ((REFS + SUB, LANES), f32), ((REFS + SUB, LANES), f32), flat,
+         ((NPTS, elems), i32), ((1, elems), i32)],
+        (pltpu.HBM,) * 4, [in_hbm(a) for a in (tracers, requests, ref_index.T, source.reshape(1, elems))],
+        [SMEM(requests.shape, i32), pltpu.SemaphoreType.DMA((3,)), pltpu.SemaphoreType.DMA((z.tiles,))],
+        flops=10**6, nbytes=10**5,
     )
     count = lax.axis_size("elem")
     to_right = [(i, (i + 1) % count) for i in range(count)]
     to_left = [((i + 1) % count, i) for i in range(count)]
     inl = lax.ppermute(payl, "elem", to_left)
     inr = lax.ppermute(payr, "elem", to_right)
-    _, parts, own, sums = call(
-        prep_kernel, z, "prep",
-        [((z.nv, width, LANES), f32), ((3, width, z.cols), bf16), ((width, z.cols), f32), ((REFS * z.tracers, LANES), f32)],
-        (VMEM, VMEM), (flat, codes), flops=10**8, nbytes=4 * 10**6,
+    parts, own, sums, codes, coef = call(
+        prep_kernel, z,
+        [((3, width, z.cols), bf16), ((width, z.cols), f32), ((REFS * z.tracers, LANES), f32), ((SUB, z.cols), i32),
+         ((NPTS * NPTS, LANES), f32)],
+        (VMEM,) * 3, (raw, refs, own_source), [VMEM((z.nv, width, LANES), f32)], flops=10**8, nbytes=4 * 10**6,
     )
     mass, tol, tor = call(
-        serve_kernel, z, "serve",
+        serve_kernel, z,
         [((1, z.tracers), f32), ((z.part, LANES), f32), ((z.part, LANES), f32)],
         (VMEM,) * 5, (wown, inl, inr, sums, parts), [VMEM((REFS, LANES), f32)], flops=10**7, nbytes=3 * 10**6,
     )
@@ -293,12 +330,12 @@
     spread = jnp.broadcast_to(mass[None], (members, 1, z.tracers))
     every = lax.all_to_all(spread, axes, 0, 0)
     (shaped,) = call(
-        final_kernel, z, "final",
-        [((elems * levels * z.tiles, LANES), f32)],
+        final_kernel, z,
+        [((elems, levels, width), f32)],
         (VMEM,) * 5, (own, froml, fromr, codes, coef),
-        [VMEM((z.nv, width, LANES), f32), VMEM((z.nv, LANES, LANES), f32)], flops=10**8, nbytes=3 * 10**6,
+        [VMEM((z.nv, width, LANES), f32), VMEM((z.nv, LANES, LANES), f32), VMEM(*flat), pltpu.SemaphoreType.DMA((z.tiles,))],
+        flops=10**8, nbytes=3 * 10**6,
     )
-    shaped = shaped.reshape(elems, z.tiles, levels, LANES).transpose(0, 2, 1, 3).reshape(elems, levels, width)
     global_mass = every.sum(axis=(0, 1))
     whole_weight = 36.0 * 4.0 * elems * count * levels * lax.axis_size("lev")
     factor = target_mean * whole_weight / global_mass
@@ -307,6 +344,5 @@
 
 def solution(mesh):
     placed = (P("elem", "lev", None), P("elem", None), P("elem", None, None), P("elem"), P())
-    return jax.shard_map(
-        per_device, mesh=mesh, in_specs=placed, out_specs=P("elem", "lev", None), check_vma=False
-    )
+
+    return jax.shard_map(per_device, mesh=mesh, in_specs=placed, out_specs=P("elem", "lev", None), check_vma=False)

time: 38.4 us -> 25.9 us (0.67)
  local copies, waits for them, and re-layouts: 7.84 us -> 0.77 us
  Pallas kernels: 12 us -> 5.26 us
  waiting for transfers between devices: 3.73 us -> 7.43 us
  starting transfers between devices: 13.9 us -> 11 us
  other arithmetic: 0.07 us -> 0.98 us
    pallas_call x4, Pallas kernels: 12 us -> 5.26 us  [call(): pl.pallas_call(functools.partial(kernel, z), out_shape=[jax.ShapeDtypeStr...]
    ppermute x1, waiting for transfers between devices: 0.01 us -> 3.54 us  [per_device(): inr = lax.ppermute(payr, 'elem', to_right)]
    all_to_all x1, starting transfers between devices: 5.79 us -> 2.81 us  [per_device(): every = lax.all_to_all(spread, axes, 0, 0)]
    unnamed x11 -> x2, local copies, waits for them, and re-layouts: 2.44 us -> 0.01 us
    reshape x3 -> x0, local copies, waits for them, and re-layouts: 1.5 us -> none  [the longest x2 1.4 us: per_device(): shaped.reshape(elems, z.tiles, levels, LANES).transpose(0, 2, 1, 3)]
    mul x2 -> x1, local copies, waits for them, and re-layouts: 1.34 us -> 0.08 us  [per_device(): return shaped * jnp.repeat(factor, NPTS)[None, None, :]]
    transpose x1 -> x0, local copies, waits for them, and re-layouts: 1.26 us -> none  [per_device(): tracers.reshape(elems, levels, z.tiles, LANES).transpose(0, 2, 1, 3)]
    mul x1, other arithmetic: 0.05 us -> 0.95 us  [per_device(): return shaped * jnp.repeat(factor, NPTS)[None, None, :]]
  transfers between devices with their start and end apart: 5 -> 5, of which waited for: 1 -> 3; matrix products, arithmetic and copies ran while one was open for 7% -> 1% of each run, Pallas kernels for 10% -> 6%
where the time goes in v2:
time: 25.9 us; the launch traced here: 25.5 us
  starting transfers between devices  11 us (42%)
  waiting for transfers between devices  7.43 us (29%)
  Pallas kernels  5.26 us (20%)
  other arithmetic  0.98 us (4%)
  local copies, waits for them, and re-layouts  0.77 us (3%)
    pallas_call x4, Pallas kernels, call(): pl.pallas_call(functools.partial(kernel, z), out_shape=[jax.ShapeDtypeStr...  5.26 us
    ppermute x1, starting transfers between devices, per_device(): inl = lax.ppermute(payl, 'elem', to_left)  4.57 us
    all_to_all x1, waiting for transfers between devices, per_device(): every = lax.all_to_all(spread, axes, 0, 0)  3.66 us
    ppermute x1, waiting for transfers between devices, per_device(): inr = lax.ppermute(payr, 'elem', to_right)  3.54 us
    ppermute x1, starting transfers between devices, per_device(): fromr = lax.ppermute(tol, 'elem', to_left)  3.29 us
    all_to_all x1, starting transfers between devices, per_device(): every = lax.all_to_all(spread, axes, 0, 0)  2.81 us
    mul x1, other arithmetic, per_device(): return shaped * jnp.repeat(factor, NPTS)[None, None, :]  0.95 us
    broadcast_in_dim x1, local copies, waits for them, and re-layouts, per_device(): spread = jnp.broadcast_to(mass[None], (members, 1, z.tracers))  0.61 us
  transfers between devices with their start and end apart: 5, of which 3 were waited for; matrix products, arithmetic and copies ran while one was open for 1% of the time, Pallas kernels for 6%

profile of v2, /device:TPU:0, one launch (start us, length us, event | category | flops | bytes accessed | tf_op | source)
XLA Modules:
  0.0 25.5 jit_solution(1306389457738059103)
XLA Ops:
  0.0 1.3 %shard_map.55 = (f32[64,128]{1,0:T(8,128)S(1)}, f32[72,128]{1,0:T(8,128)S(1)}, f32[72,128]{1,0:T(8,128)S(1)}, f32[5,256,128]{2,1,0:T(8,128)S(1)}, s32[16,64]{1,0:T(8,128)S(1)}, /*index=5*/s32[1,64]{1,0:T(1,128)S(1)}) custom-call(f32[64,4,640]{2,1,0:T(4,128)} %x_hbm.1, s32[1,2,16]{2,1,0:T(2,128)} %req_hbm.1, s32[16,64]{1,0:T(8,128)} %bitcast.6, s32[1,64]{1,0:T(1,128)} %bitcast.7), custom_call_target="tpu_custom_call" | custom-call | flops 1000000 | bytes 100000 | tf_op jit(solution)/shard_map/pallas_call | solution.py:284
  1.3 4.6 %collective-permute-start = (f32[72,128]{1,0:T(8,128)S(1)}, f32[72,128]{1,0:T(8,128)S(1)}, u32[]{:S(2)}, u32[]{:S(2)}) collective-permute-start(f32[72,128]{1,0:T(8,128)S(1)} %get-tuple-element.24), channel_id=1, source_target_pairs={{4,0},{8,4},{12,8},{16,12},{20,16},{24,20},{28,24},{0,28},{5,1},{9... | collective-permute-start | bytes 110600 | tf_op jit(solution)/shard_map/ppermute | solution.py:313
  5.9 0.0 collective-permute-start.1
  5.9 1.4 %shard_map.56 = (bf16[3,640,256]{2,1,0:T(8,128)(2,1)S(1)}, f32[640,256]{1,0:T(8,128)S(1)}, f32[2560,128]{1,0:T(8,128)S(1)}, s32[8,256]{1,0:T(8,128)S(1)}, f32[256,128]{1,0:T(8,128)S(1)}) custom-call(f32[5,256,128]{2,1,0:T(8,128)S(1)} %get-tuple-element.19.raw_ref, s32[16,64]{1,0:T(8,128)S(1)} %get-tuple-element.20.ref_ref, s32[1,64]{1,0:T(1,128)S(1)} %get-tuple-element.21.src_ref), custom_call_target="tpu_custom_call" | custom-call | flops 100000000 | bytes 4000000 | tf_op jit(solution)/shard_map/pallas_call | solution.py:284
  7.3 0.0 copy-start
  7.3 0.2 collective-permute-done.inl_ref
  7.5 3.5 %collective-permute-done.1.inr_ref = f32[72,128]{1,0:T(8,128)S(1)} collective-permute-done((f32[72,128]{1,0:T(8,128)S(1)}, f32[72,128]{1,0:T(8,128)S(1)}, u32[]{:S(2)}, u32[]{:S(2)}) %collective-permute-start.1) | collective-permute-done | bytes 36896 | tf_op jit(solution)/shard_map/ppermute | solution.py:314
  11.0 0.5 %shard_map.57 = (f32[1,40]{1,0:T(1,128)S(1)}, f32[320,128]{1,0:T(8,128)S(1)}, f32[320,128]{1,0:T(8,128)S(1)}) custom-call(f32[64,128]{1,0:T(8,128)S(1)} %get-tuple-element.23.wown_ref, f32[72,128]{1,0:T(8,128)S(1)} %collective-permute-done.inl_ref, f32[72,128]{1,0:T(8,128)S(1)} %collective-permute-done.1.inr_ref, ...), custom_call_target="tpu_custom_call" | custom-call | flops 10000000 | bytes 3000000 | tf_op jit(solution)/shard_map/pallas_call | solution.py:284
  11.6 0.6 %broadcast_in_dim.12 = f32[32,1,40]{2,1,0:T(1,128)} broadcast(f32[40]{0:T(128)S(1)} %bitcast.4), dimensions={2} | broadcast | bytes 5280 | tf_op jit(solution)/shard_map/broadcast_in_dim | solution.py:330
  12.2 2.8 %all-to-all-start = ((f32[32,1,40]{2,1,0:T(1,128)}), f32[32,1,40]{2,1,0:T(1,128)S(1)}, u32[]{:S(2)}, u32[]{:S(2)}) async-start(f32[32,1,40]{2,1,0:T(1,128)} %broadcast_in_dim.12), calls=%async_computation | async-start | bytes 32768 | tf_op jit(solution)/shard_map/all_to_all | solution.py:331
  15.0 0.3 %collective-permute-start.2 = (f32[320,128]{1,0:T(8,128)S(1)}, f32[320,128]{1,0:T(8,128)S(1)}, u32[]{:S(2)}, u32[]{:S(2)}) collective-permute-start(f32[320,128]{1,0:T(8,128)S(1)} %get-tuple-element.28), channel_id=1, source_target_pairs={{0,4},{4,8},{8,12},{12,16},{16,20},{20,24},{24,28},{28,0},{1,5},{5... | collective-permute-start | bytes 491528 | tf_op jit(solution)/shard_map/ppermute | solution.py:326
  15.3 3.3 %collective-permute-start.3 = (f32[320,128]{1,0:T(8,128)S(1)}, f32[320,128]{1,0:T(8,128)S(1)}, u32[]{:S(2)}, u32[]{:S(2)}) collective-permute-start(f32[320,128]{1,0:T(8,128)S(1)} %get-tuple-element.29), channel_id=1, source_target_pairs={{4,0},{8,4},{12,8},{16,12},{20,16},{24,20},{28,24},{0,28},{5,1},{9... | collective-permute-start | bytes 491528 | tf_op jit(solution)/shard_map/ppermute | solution.py:327
  18.6 3.7 %all-to-all-done = f32[32,1,40]{2,1,0:T(1,128)S(1)} async-done(((f32[32,1,40]{2,1,0:T(1,128)}), f32[32,1,40]{2,1,0:T(1,128)S(1)}, u32[]{:S(2)}, u32[]{:S(2)}) %all-to-all-start) | async-done | bytes 5152 | tf_op jit(solution)/shard_map/all_to_all | solution.py:331
  22.3 0.0 copy-done
  22.3 0.1 broadcast_in_dim.13
  22.4 0.1 mul.18
  22.4 0.0 collective-permute-done.2.froml_ref
  22.4 0.0 collective-permute-done.3.fromr_ref
  22.4 2.1 %shard_map.58 = f32[64,4,640]{2,1,0:T(4,128)S(1)} custom-call(f32[640,256]{1,0:T(8,128)S(1)} %get-tuple-element.22.own_ref, f32[320,128]{1,0:T(8,128)S(1)} %collective-permute-done.2.froml_ref, f32[320,128]{1,0:T(8,128)S(1)} %collective-permute-done.3.fromr_ref, s32[8,256]{1,0:T(8,128)S(1)} %get-tuple-element.30.codes_ref, ...), custom_call_target="tpu_custom_call" | custom-call | flops 100000000 | bytes 3000000 | tf_op jit(solution)/shard_map/pallas_call | solution.py:284
  24.5 1.0 %broadcast_multiply_fusion = f32[64,4,640]{2,1,0:T(4,128)} fusion(f32[64,4,640]{2,1,0:T(4,128)S(1)} %shard_map.58, f32[640]{0:T(1024)S(1)} %mul.18), kind=kLoop, calls=%fused_computation | loop fusion | flops 163840 | bytes 1313280 | tf_op jit(solution)/shard_map/mul | solution.py:342
  (2 shorter events, 0.0 us)
Async XLA Ops:
  1.3 6.2 %collective-permute-start = (f32[72,128]{1,0:T(8,128)S(1)}, f32[72,128]{1,0:T(8,128)S(1)}, u32[]{:S(2)}, u32[]{:S(2)}) collective-permute-start(f32[72,128]{1,0:T(8,128)S(1)} %get-tuple-element.24), channel_id=1, source_target_pairs={{4,0},{8,4},{12,8},{16,12},{20,16},{24,20},{28,24},{0,28},{5,1},{9... | collective-permute-start | bytes 110600 | tf_op jit(solution)/shard_map/ppermute | solution.py:313
  5.9 5.2 %collective-permute-start.1 = (f32[72,128]{1,0:T(8,128)S(1)}, f32[72,128]{1,0:T(8,128)S(1)}, u32[]{:S(2)}, u32[]{:S(2)}) collective-permute-start(f32[72,128]{1,0:T(8,128)S(1)} %get-tuple-element.25), channel_id=1, source_target_pairs={{0,4},{4,8},{8,12},{12,16},{16,20},{20,24},{24,28},{28,0},{1,5},{5... | collective-permute-start | bytes 110600 | tf_op jit(solution)/shard_map/ppermute | solution.py:314
  7.3 15.0 %copy-start = (f32[40]{0:T(128)S(1)}, f32[40]{0:T(128)}, u32[]{:S(2)}) copy-start(f32[40]{0:T(128)} %param.9) | copy-start | bytes 484
  12.2 10.1 %all-to-all-start = ((f32[32,1,40]{2,1,0:T(1,128)}), f32[32,1,40]{2,1,0:T(1,128)S(1)}, u32[]{:S(2)}, u32[]{:S(2)}) async-start(f32[32,1,40]{2,1,0:T(1,128)} %broadcast_in_dim.12), calls=%async_computation | async-start | bytes 32768 | tf_op jit(solution)/shard_map/all_to_all | solution.py:331
  15.0 7.4 %collective-permute-start.2 = (f32[320,128]{1,0:T(8,128)S(1)}, f32[320,128]{1,0:T(8,128)S(1)}, u32[]{:S(2)}, u32[]{:S(2)}) collective-permute-start(f32[320,128]{1,0:T(8,128)S(1)} %get-tuple-element.28), channel_id=1, source_target_pairs={{0,4},{4,8},{8,12},{12,16},{16,20},{20,24},{24,28},{28,0},{1,5},{5... | collective-permute-start | bytes 491528 | tf_op jit(solution)/shard_map/ppermute | solution.py:326
  15.3 7.1 %collective-permute-start.3 = (f32[320,128]{1,0:T(8,128)S(1)}, f32[320,128]{1,0:T(8,128)S(1)}, u32[]{:S(2)}, u32[]{:S(2)}) collective-permute-start(f32[320,128]{1,0:T(8,128)S(1)} %get-tuple-element.29), channel_id=1, source_target_pairs={{4,0},{8,4},{12,8},{16,12},{20,16},{24,20},{28,24},{0,28},{5,1},{9... | collective-permute-start | bytes 491528 | tf_op jit(solution)/shard_map/ppermute | solution.py:327

commit v3 on v2

--- a/solution.py
+++ b/solution.py
@@ -68,7 +68,7 @@
 
 
 def plan_kernel(
-    z, x_hbm, req_hbm, ref_hbm, src_hbm, wown_ref, payl_ref, payr_ref, raw_ref, ref_ref, src_ref, req_ref, sem, xsem
+    z, x_hbm, req_hbm, ref_hbm, src_hbm, wown_ref, far_ref, near_ref, raw_ref, ref_ref, src_ref, req_ref, sem, xsem
 ):
     elems, slots = z.elems, z.slots
     small = [
@@ -88,16 +88,18 @@
     src = src_ref[...]
     lane = lax.broadcasted_iota(jnp.int32, (1, LANES), 1)
     k_lane = lane % slots
-    first = jnp.full((1, elems), -1, jnp.int32)
-    second = first
-    pat_l = jnp.zeros((1, LANES), jnp.int32)
-    pat_r = pat_l
+    odd = lax.rem(lax.axis_index("elem"), 2)
+    far_base, near_base = elems + odd * slots, elems + (1 - odd) * slots
+    far = jnp.full((1, elems), -1, jnp.int32)
+    near = far
+    pat_far = jnp.zeros((1, LANES), jnp.int32)
+    pat_near = pat_far
     for k in range(slots):
-        left, right = req_ref[0, 0, k], req_ref[0, 1, k]
-        first = jnp.where(src == elems + k, left, first)
-        second = jnp.where(src == elems + slots + k, right, second)
-        pat_l = jnp.where(k_lane == k, left, pat_l)
-        pat_r = jnp.where(k_lane == k, right, pat_r)
+        far_k, near_k = req_ref[0, odd, k], req_ref[0, 1 - odd, k]
+        far = jnp.where(src == far_base + k, far_k, far)
+        near = jnp.where(src == near_base + k, near_k, near)
+        pat_far = jnp.where(k_lane == k, far_k, pat_far)
+        pat_near = jnp.where(k_lane == k, near_k, pat_near)
     ref = ref_ref[...]
     row = lax.broadcasted_iota(jnp.int32, (REFS, elems), 0)
     counts = jnp.zeros((REFS, elems), jnp.float32)
@@ -110,16 +112,17 @@
         return mm_nt(counts, (srow == which).astype(jnp.float32).astype(jnp.bfloat16))
 
     wown_ref[...] = weights(src)
-    payl_ref[0:REFS, :] = weights(first)
-    payl_ref[REFS : REFS + SUB, :] = jnp.broadcast_to(pat_l.astype(jnp.float32), (SUB, LANES))
-    payr_ref[0:REFS, :] = weights(second)
-    payr_ref[REFS : REFS + SUB, :] = jnp.broadcast_to(pat_r.astype(jnp.float32), (SUB, LANES))
+    far_ref[0:REFS, :] = weights(far)
+    far_ref[REFS : REFS + SUB, :] = jnp.broadcast_to(pat_far.astype(jnp.float32), (SUB, LANES))
+    near_ref[0:REFS, :] = weights(near)
+    near_ref[REFS : REFS + SUB, :] = jnp.broadcast_to(pat_near.astype(jnp.float32), (SUB, LANES))
     for copy in large:
         copy.wait()
 
 
 def tables(z, src, ref, codes_ref, coef_ref):
     elems, slots, levels = z.elems, z.slots, z.levels
+    odd = lax.rem(lax.axis_index("elem"), 2)
     lane = lax.broadcasted_iota(jnp.int32, (1, LANES), 1)
     src2 = jnp.concatenate([src] * z.per, axis=1)
     sub_level = lane // elems
@@ -129,7 +132,7 @@
         codes_ref[0:1, at] = jnp.where(src2 < elems, level * elems + src2, -1)
         rel = src2 - elems
         side = jnp.where(rel >= slots, 1, 0)
-        code = side * LANES + level * slots + (rel - side * slots)
+        code = jnp.where(side == odd, 0, LANES) + level * slots + (rel - side * slots)
         for h in range(z.halves):
             codes_ref[1 + h : 2 + h, at] = jnp.where(rel >= 0, code + h * levels * slots, -1)
 
@@ -204,12 +207,12 @@
             sums_ref[r * z.tracers + j * z.tpt : r * z.tracers + (j + 1) * z.tpt, :] = both[r]
 
 
-def serve_kernel(z, wown_ref, inl_ref, inr_ref, sums_ref, parts_ref, mass_ref, tol_ref, tor_ref, weight_ref):
-    weight_ref[...] = wown_ref[...] + inl_ref[0:REFS, :] + inr_ref[0:REFS, :]
+def serve_kernel(z, wown_ref, infar_ref, innear_ref, sums_ref, parts_ref, mass_ref, tofar_ref, tonear_ref, weight_ref):
+    weight_ref[...] = wown_ref[...] + infar_ref[0:REFS, :] + innear_ref[0:REFS, :]
     lane = lax.broadcasted_iota(jnp.int32, (1, LANES), 1)
     level = (lane // z.slots) % z.levels
     codes = []
-    for ref in (inl_ref, inr_ref):
+    for ref in (infar_ref, innear_ref):
         wanted = ref[REFS : REFS + 1, :].astype(jnp.int32)
         codes.append(jnp.where(wanted >= 0, level * z.elems + wanted, -1))
     code = jnp.concatenate(codes, axis=1)
@@ -217,7 +220,7 @@
     pick = (row == code).astype(jnp.float32).astype(jnp.bfloat16)
     rows = onehot_dot((parts_ref[0], parts_ref[1], parts_ref[2]), pick)
     half = lane // (z.levels * z.slots)
-    for ref, at in ((tor_ref, slice(0, LANES)), (tol_ref, slice(LANES, 2 * LANES))):
+    for ref, at in ((tofar_ref, slice(0, LANES)), (tonear_ref, slice(LANES, 2 * LANES))):
         value = rows[0 : z.part, at]
         for h in range(1, z.halves):
             value = jnp.where(half == h, rows[h * z.part : (h + 1) * z.part, at], value)
@@ -232,11 +235,12 @@
     total = jnp.concatenate(total, axis=0)
     ones = jnp.ones((SUB, LANES), jnp.bfloat16)
     parts = split3(total)
-    mass_ref[...] = sum(mm_nt(ones, part) for part in parts)[0:1, :]
-
-
-def final_kernel(z, own_ref, froml_ref, fromr_ref, codes_ref, coef_ref, out_ref, got_ref, turn_ref, flat_ref, sem):
-    halo = jnp.concatenate([froml_ref[...], fromr_ref[...]], axis=1)
+    mass = sum(mm_nt(ones, part) for part in parts)[0:1, :]
+    mass_ref[...] = jnp.broadcast_to(mass[None], mass_ref.shape)
+
+
+def final_kernel(z, own_ref, far_ref, near_ref, codes_ref, coef_ref, out_ref, got_ref, turn_ref, flat_ref, sem):
+    halo = jnp.concatenate([far_ref[...], near_ref[...]], axis=1)
     parts = split3(halo)
     row = lax.broadcasted_iota(jnp.int32, (2 * LANES, z.cols), 0)
     for h in range(z.halves):
@@ -299,7 +303,7 @@
     assert z.halves * levels * z.slots == LANES and z.part * z.halves == width
     f32, bf16, i32 = jnp.float32, jnp.bfloat16, jnp.int32
     flat = ((z.tiles, elems * levels, LANES), f32)
-    wown, payl, payr, raw, refs, own_source = call(
+    wown, ask_far, ask_near, raw, refs, own_source = call(
         plan_kernel, z,
         [((REFS, LANES), f32), ((REFS + SUB, LANES), f32), ((REFS + SUB, LANES), f32), flat,
          ((NPTS, elems), i32), ((1, elems), i32)],
@@ -308,31 +312,30 @@
         flops=10**6, nbytes=10**5,
     )
     count = lax.axis_size("elem")
-    to_right = [(i, (i + 1) % count) for i in range(count)]
-    to_left = [((i + 1) % count, i) for i in range(count)]
-    inl = lax.ppermute(payl, "elem", to_left)
-    inr = lax.ppermute(payr, "elem", to_right)
+    assert count % 2 == 0
+    far = [(i, (i - 1 if i % 2 == 0 else i + 1) % count) for i in range(count)]
+    near = [(i, i + 1 if i % 2 == 0 else i - 1) for i in range(count)]
+    in_far = lax.ppermute(ask_far, "elem", far)
+    in_near = lax.ppermute(ask_near, "elem", near)
     parts, own, sums, codes, coef = call(
         prep_kernel, z,
         [((3, width, z.cols), bf16), ((width, z.cols), f32), ((REFS * z.tracers, LANES), f32), ((SUB, z.cols), i32),
          ((NPTS * NPTS, LANES), f32)],
         (VMEM,) * 3, (raw, refs, own_source), [VMEM((z.nv, width, LANES), f32)], flops=10**8, nbytes=4 * 10**6,
     )
-    mass, tol, tor = call(
+    axes = ("elem", "lev")
+    spread, to_far, to_near = call(
         serve_kernel, z,
-        [((1, z.tracers), f32), ((z.part, LANES), f32), ((z.part, LANES), f32)],
-        (VMEM,) * 5, (wown, inl, inr, sums, parts), [VMEM((REFS, LANES), f32)], flops=10**7, nbytes=3 * 10**6,
+        [((lax.axis_size(axes), 1, z.tracers), f32), ((z.part, LANES), f32), ((z.part, LANES), f32)],
+        (VMEM,) * 5, (wown, in_far, in_near, sums, parts), [VMEM((REFS, LANES), f32)], flops=10**7, nbytes=3 * 10**6,
     )
-    froml = lax.ppermute(tor, "elem", to_right)
-    fromr = lax.ppermute(tol, "elem", to_left)
-    axes = ("elem", "lev")
-    members = lax.axis_size(axes)
-    spread = jnp.broadcast_to(mass[None], (members, 1, z.tracers))
+    from_far = lax.ppermute(to_far, "elem", far)
+    from_near = lax.ppermute(to_near, "elem", near)
     every = lax.all_to_all(spread, axes, 0, 0)
     (shaped,) = call(
         final_kernel, z,
         [((elems, levels, width), f32)],
-        (VMEM,) * 5, (own, froml, fromr, codes, coef),
+        (VMEM,) * 5, (own, from_far, from_near, codes, coef),
         [VMEM((z.nv, width, LANES), f32), VMEM((z.nv, LANES, LANES), f32), VMEM(*flat), pltpu.SemaphoreType.DMA((z.tiles,))],
         flops=10**8, nbytes=3 * 10**6,
     )

time: 25.9 us -> 25.7 us (level)
  waiting for transfers between devices: 7.43 us -> 4.71 us
  starting transfers between devices: 11 us -> 13.7 us
  Pallas kernels: 5.26 us -> 5.88 us
  local copies, waits for them, and re-layouts: 0.77 us -> 0.15 us
    all_to_all x1, starting transfers between devices: 2.81 us -> 5.68 us  [per_device(): every = lax.all_to_all(spread, axes, 0, 0)]
    ppermute x4, waiting for transfers between devices: 3.76 us -> 0.9 us  [the longest x1 0.58 us: per_device(): from_far = lax.ppermute(to_far, 'elem', far)]
    pallas_call x4, Pallas kernels: 5.26 us -> 5.88 us  [call(): pl.pallas_call(functools.partial(kernel, z), out_shape=[jax.ShapeDtypeStr...]
    broadcast_in_dim x1 -> x0, local copies, waits for them, and re-layouts: 0.61 us -> none  [per_device(): spread = jnp.broadcast_to(mass[None], (members, 1, z.tracers))]
where the time goes in v3:
time: 25.7 us; the launch traced here: 25.5 us
  starting transfers between devices  13.7 us (53%)
  Pallas kernels  5.88 us (23%)
  waiting for transfers between devices  4.71 us (18%)
  other arithmetic  1.01 us (4%)
    pallas_call x4, Pallas kernels, call(): pl.pallas_call(functools.partial(kernel, z), out_shape=[jax.ShapeDtypeStr...  5.88 us
    all_to_all x1, starting transfers between devices, per_device(): every = lax.all_to_all(spread, axes, 0, 0)  5.68 us
    ppermute x1, starting transfers between devices, per_device(): in_far = lax.ppermute(ask_far, 'elem', far)  4.58 us
    all_to_all x1, waiting for transfers between devices, per_device(): every = lax.all_to_all(spread, axes, 0, 0)  3.81 us
    ppermute x1, starting transfers between devices, per_device(): from_far = lax.ppermute(to_far, 'elem', far)  3.41 us
    mul x1, other arithmetic, per_device(): return shaped * jnp.repeat(factor, NPTS)[None, None, :]  0.95 us
    ppermute x1, waiting for transfers between devices, per_device(): from_far = lax.ppermute(to_far, 'elem', far)  0.58 us
  transfers between devices with their start and end apart: 5, of which 3 were waited for; matrix products, arithmetic and copies ran while one was open for 1% of the time, Pallas kernels for 6%

profile of v3, /device:TPU:0, one launch (start us, length us, event | category | flops | bytes accessed | tf_op | source)
XLA Modules:
  0.0 25.5 jit_solution(3652677957477269678)
XLA Ops:
  0.0 1.3 %shard_map.55 = (f32[64,128]{1,0:T(8,128)S(1)}, f32[72,128]{1,0:T(8,128)S(1)}, f32[72,128]{1,0:T(8,128)S(1)}, f32[5,256,128]{2,1,0:T(8,128)S(1)}, s32[16,64]{1,0:T(8,128)S(1)}, /*index=5*/s32[1,64]{1,0:T(1,128)S(1)}) custom-call(f32[64,4,640]{2,1,0:T(4,128)} %x_hbm.1, s32[1,2,16]{2,1,0:T(2,128)} %req_hbm.1, s32[16,64]{1,0:T(8,128)} %bitcast.2, s32[1,64]{1,0:T(1,128)} %bitcast.3), custom_call_target="tpu_custom_call" | custom-call | flops 1000000 | bytes 100000 | tf_op jit(solution)/shard_map/pallas_call | solution.py:288
  1.3 4.6 %collective-permute-start = (f32[72,128]{1,0:T(8,128)S(1)}, f32[72,128]{1,0:T(8,128)S(1)}, u32[]{:S(2)}, u32[]{:S(2)}) collective-permute-start(f32[72,128]{1,0:T(8,128)S(1)} %get-tuple-element.24), channel_id=1, source_target_pairs={{0,28},{4,8},{8,4},{12,16},{16,12},{20,24},{24,20},{28,0},{1,29},{... | collective-permute-start | bytes 110600 | tf_op jit(solution)/shard_map/ppermute | solution.py:318
  5.9 0.0 collective-permute-start.1
  5.9 1.4 %shard_map.56 = (bf16[3,640,256]{2,1,0:T(8,128)(2,1)S(1)}, f32[640,256]{1,0:T(8,128)S(1)}, f32[2560,128]{1,0:T(8,128)S(1)}, s32[8,256]{1,0:T(8,128)S(1)}, f32[256,128]{1,0:T(8,128)S(1)}) custom-call(f32[5,256,128]{2,1,0:T(8,128)S(1)} %get-tuple-element.19.raw_ref, s32[16,64]{1,0:T(8,128)S(1)} %get-tuple-element.20.ref_ref, s32[1,64]{1,0:T(1,128)S(1)} %get-tuple-element.21.src_ref), custom_call_target="tpu_custom_call" | custom-call | flops 100000000 | bytes 4000000 | tf_op jit(solution)/shard_map/pallas_call | solution.py:288
  7.3 0.0 copy-start
  7.3 0.3 %collective-permute-done.infar_ref = f32[72,128]{1,0:T(8,128)S(1)} collective-permute-done((f32[72,128]{1,0:T(8,128)S(1)}, f32[72,128]{1,0:T(8,128)S(1)}, u32[]{:S(2)}, u32[]{:S(2)}) %collective-permute-start) | collective-permute-done | bytes 36896 | tf_op jit(solution)/shard_map/ppermute | solution.py:318
  7.6 0.0 collective-permute-done.1.innear_ref
  7.6 1.1 %shard_map.57 = (f32[32,1,40]{2,1,0:T(1,128)}, f32[320,128]{1,0:T(8,128)S(1)}, f32[320,128]{1,0:T(8,128)S(1)}) custom-call(f32[64,128]{1,0:T(8,128)S(1)} %get-tuple-element.23.wown_ref, f32[72,128]{1,0:T(8,128)S(1)} %collective-permute-done.infar_ref, f32[72,128]{1,0:T(8,128)S(1)} %collective-permute-done.1.innear_ref, ...), custom_call_target="tpu_custom_call" | custom-call | flops 10000000 | bytes 3000000 | tf_op jit(solution)/shard_map/pallas_call | solution.py:288
  8.7 5.7 %all-to-all-start = ((f32[32,1,40]{2,1,0:T(1,128)}), f32[32,1,40]{2,1,0:T(1,128)S(1)}, u32[]{:S(2)}, u32[]{:S(2)}) async-start(f32[32,1,40]{2,1,0:T(1,128)} %get-tuple-element.32), calls=%async_computation | async-start | bytes 32768 | tf_op jit(solution)/shard_map/all_to_all | solution.py:334
  14.4 3.4 %collective-permute-start.2 = (f32[320,128]{1,0:T(8,128)S(1)}, f32[320,128]{1,0:T(8,128)S(1)}, u32[]{:S(2)}, u32[]{:S(2)}) collective-permute-start(f32[320,128]{1,0:T(8,128)S(1)} %get-tuple-element.28), channel_id=1, source_target_pairs={{0,28},{4,8},{8,4},{12,16},{16,12},{20,24},{24,20},{28,0},{1,29},{... | collective-permute-start | bytes 491528 | tf_op jit(solution)/shard_map/ppermute | solution.py:332
  17.8 0.0 collective-permute-start.3
  17.9 3.8 %all-to-all-done = f32[32,1,40]{2,1,0:T(1,128)S(1)} async-done(((f32[32,1,40]{2,1,0:T(1,128)}), f32[32,1,40]{2,1,0:T(1,128)S(1)}, u32[]{:S(2)}, u32[]{:S(2)}) %all-to-all-start) | async-done | bytes 5152 | tf_op jit(solution)/shard_map/all_to_all | solution.py:334
  21.7 0.1 reduce_sum.9
  21.7 0.0 copy-done
  21.7 0.1 broadcast_in_dim.3
  21.8 0.1 mul.18
  21.9 0.6 %collective-permute-done.2.far_ref = f32[320,128]{1,0:T(8,128)S(1)} collective-permute-done((f32[320,128]{1,0:T(8,128)S(1)}, f32[320,128]{1,0:T(8,128)S(1)}, u32[]{:S(2)}, u32[]{:S(2)}) %collective-permute-start.2) | collective-permute-done | bytes 163872 | tf_op jit(solution)/shard_map/ppermute | solution.py:332
  22.5 0.0 collective-permute-done.3.near_ref
  22.5 2.1 %shard_map.58 = f32[64,4,640]{2,1,0:T(4,128)S(1)} custom-call(f32[640,256]{1,0:T(8,128)S(1)} %get-tuple-element.22.own_ref, f32[320,128]{1,0:T(8,128)S(1)} %collective-permute-done.2.far_ref, f32[320,128]{1,0:T(8,128)S(1)} %collective-permute-done.3.near_ref, s32[8,256]{1,0:T(8,128)S(1)} %get-tuple-element.30.codes_ref, ...), custom_call_target="tpu_custom_call" | custom-call | flops 100000000 | bytes 3000000 | tf_op jit(solution)/shard_map/pallas_call | solution.py:288
  24.5 1.0 %broadcast_multiply_fusion = f32[64,4,640]{2,1,0:T(4,128)} fusion(f32[64,4,640]{2,1,0:T(4,128)S(1)} %shard_map.58, f32[640]{0:T(1024)S(1)} %mul.18), kind=kLoop, calls=%fused_computation | loop fusion | flops 163840 | bytes 1313280 | tf_op jit(solution)/shard_map/mul | solution.py:345
  (1 shorter events, 0.0 us)
Async XLA Ops:
  1.3 6.3 %collective-permute-start = (f32[72,128]{1,0:T(8,128)S(1)}, f32[72,128]{1,0:T(8,128)S(1)}, u32[]{:S(2)}, u32[]{:S(2)}) collective-permute-start(f32[72,128]{1,0:T(8,128)S(1)} %get-tuple-element.24), channel_id=1, source_target_pairs={{0,28},{4,8},{8,4},{12,16},{16,12},{20,24},{24,20},{28,0},{1,29},{... | collective-permute-start | bytes 110600 | tf_op jit(solution)/shard_map/ppermute | solution.py:318
  5.9 1.7 %collective-permute-start.1 = (f32[72,128]{1,0:T(8,128)S(1)}, f32[72,128]{1,0:T(8,128)S(1)}, u32[]{:S(2)}, u32[]{:S(2)}) collective-permute-start(f32[72,128]{1,0:T(8,128)S(1)} %get-tuple-element.25), channel_id=1, source_target_pairs={{0,4},{4,0},{8,12},{12,8},{16,20},{20,16},{24,28},{28,24},{1,5},{5... | collective-permute-start | bytes 110600 | tf_op jit(solution)/shard_map/ppermute | solution.py:319
  7.3 14.4 %copy-start = (f32[40]{0:T(128)S(1)}, f32[40]{0:T(128)}, u32[]{:S(2)}) copy-start(f32[40]{0:T(128)} %param.9) | copy-start | bytes 484
  8.7 12.9 %all-to-all-start = ((f32[32,1,40]{2,1,0:T(1,128)}), f32[32,1,40]{2,1,0:T(1,128)S(1)}, u32[]{:S(2)}, u32[]{:S(2)}) async-start(f32[32,1,40]{2,1,0:T(1,128)} %get-tuple-element.32), calls=%async_computation | async-start | bytes 32768 | tf_op jit(solution)/shard_map/all_to_all | solution.py:334
  14.4 8.0 %collective-permute-start.2 = (f32[320,128]{1,0:T(8,128)S(1)}, f32[320,128]{1,0:T(8,128)S(1)}, u32[]{:S(2)}, u32[]{:S(2)}) collective-permute-start(f32[320,128]{1,0:T(8,128)S(1)} %get-tuple-element.28), channel_id=1, source_target_pairs={{0,28},{4,8},{8,4},{12,16},{16,12},{20,24},{24,20},{28,0},{1,29},{... | collective-permute-start | bytes 491528 | tf_op jit(solution)/shard_map/ppermute | solution.py:332
  17.8 4.6 %collective-permute-start.3 = (f32[320,128]{1,0:T(8,128)S(1)}, f32[320,128]{1,0:T(8,128)S(1)}, u32[]{:S(2)}, u32[]{:S(2)}) collective-permute-start(f32[320,128]{1,0:T(8,128)S(1)} %get-tuple-element.29), channel_id=1, source_target_pairs={{0,4},{4,0},{8,12},{12,8},{16,20},{20,16},{24,28},{28,24},{1,5},{5... | collective-permute-start | bytes 491528 | tf_op jit(solution)/shard_map/ppermute | solution.py:333

commit v4 on v3

--- a/solution.py
+++ b/solution.py
@@ -65,32 +65,33 @@
         self.tpt = LANES // NPTS
         self.halves = LANES // (levels * slots)
         self.part = width // self.halves
+        self.wrows = REFS // self.per
 
 
 def plan_kernel(
-    z, x_hbm, req_hbm, ref_hbm, src_hbm, wown_ref, far_ref, near_ref, raw_ref, ref_ref, src_ref, req_ref, sem, xsem
+    z, req_hbm, ref_hbm, src_hbm, wown_ref, far_ref, near_ref, ref_ref, src_ref, req_ref, sem
 ):
     elems, slots = z.elems, z.slots
-    small = [
+    copies = [
         pltpu.make_async_copy(src, dst, sem.at[i])
         for i, (src, dst) in enumerate(((req_hbm, req_ref), (ref_hbm, ref_ref), (src_hbm, src_ref)))
     ]
-    large = [
-        pltpu.make_async_copy(
-            x_hbm.at[:, :, pl.ds(j * LANES, LANES)], raw_ref.at[j].reshape(elems, z.levels, LANES), xsem.at[j]
-        )
-        for j in range(z.tiles)
-    ]
-    for copy in small + large:
+    for copy in copies:
         copy.start()
-    for copy in small:
+    odd = lax.rem(lax.axis_index("elem"), 2)
+    lane = lax.broadcasted_iota(jnp.int32, (1, LANES), 1)
+    group = lane // elems
+    row = lax.broadcasted_iota(jnp.int32, (z.wrows, LANES), 0) + z.wrows * group
+    srow = lax.broadcasted_iota(jnp.int32, (LANES, LANES), 0)
+    k_lane = lane % slots
+    for copy in copies:
         copy.wait()
-    src = src_ref[...]
-    lane = lax.broadcasted_iota(jnp.int32, (1, LANES), 1)
-    k_lane = lane % slots
-    odd = lax.rem(lax.axis_index("elem"), 2)
+    ref = jnp.concatenate([ref_ref[...]] * z.per, axis=1)
+    counts = tree(jnp.add, [jnp.where(row == ref[p : p + 1, :], float(WEIGHT36[p]), 0.0) for p in range(NPTS)])
+    counts = counts.astype(jnp.bfloat16)
+    src = jnp.concatenate([src_ref[...]] * z.per, axis=1)
     far_base, near_base = elems + odd * slots, elems + (1 - odd) * slots
-    far = jnp.full((1, elems), -1, jnp.int32)
+    far = jnp.full((1, LANES), -1, jnp.int32)
     near = far
     pat_far = jnp.zeros((1, LANES), jnp.int32)
     pat_near = pat_far
@@ -100,24 +101,17 @@
         near = jnp.where(src == near_base + k, near_k, near)
         pat_far = jnp.where(k_lane == k, far_k, pat_far)
         pat_near = jnp.where(k_lane == k, near_k, pat_near)
-    ref = ref_ref[...]
-    row = lax.broadcasted_iota(jnp.int32, (REFS, elems), 0)
-    counts = jnp.zeros((REFS, elems), jnp.float32)
-    for p in range(NPTS):
-        counts = counts + jnp.where(row == ref[p : p + 1, :], float(WEIGHT36[p]), 0.0)
-    counts = counts.astype(jnp.bfloat16)
-    srow = lax.broadcasted_iota(jnp.int32, (LANES, elems), 0) % elems
+    own = jnp.where(src < elems, src, -1)
 
     def weights(which):
-        return mm_nt(counts, (srow == which).astype(jnp.float32).astype(jnp.bfloat16))
-
-    wown_ref[...] = weights(src)
-    far_ref[0:REFS, :] = weights(far)
-    far_ref[REFS : REFS + SUB, :] = jnp.broadcast_to(pat_far.astype(jnp.float32), (SUB, LANES))
-    near_ref[0:REFS, :] = weights(near)
-    near_ref[REFS : REFS + SUB, :] = jnp.broadcast_to(pat_near.astype(jnp.float32), (SUB, LANES))
-    for copy in large:
-        copy.wait()
+        pick = srow == jnp.where(which >= 0, which + elems * group, -1)
+        return mm_nt(counts, pick.astype(jnp.float32).astype(jnp.bfloat16))
+
+    far_ref[0 : z.wrows, :] = weights(far)
+    far_ref[z.wrows :, :] = jnp.broadcast_to(pat_far.astype(jnp.float32), (SUB, LANES))
+    near_ref[0 : z.wrows, :] = weights(near)
+    near_ref[z.wrows :, :] = jnp.broadcast_to(pat_near.astype(jnp.float32), (SUB, LANES))
+    wown_ref[...] = weights(own)
 
 
 def tables(z, src, ref, codes_ref, coef_ref):
@@ -175,7 +169,7 @@
     return values[0]
 
 
-def prep_kernel(z, raw_ref, ref_ref, src_ref, parts_ref, own_ref, sums_ref, codes_ref, coef_ref, xt_ref):
+def prep_kernel(z, x_ref, ref_ref, src_ref, parts_ref, own_ref, sums_ref, codes_ref, coef_ref, xt_ref):
     tables(z, src_ref[...], ref_ref[...], codes_ref, coef_ref)
     for j in range(z.tiles):
         for v in range(z.nv):
@@ -183,7 +177,7 @@
             for q in range(z.per):
                 level = v * z.per + q
                 for e in range(0, z.elems, SUB):
-                    rows.append(raw_ref[j, pl.ds(e * z.levels + level, SUB, stride=z.levels), :])
+                    rows.append(x_ref[pl.ds(e, SUB), level, pl.ds(j * LANES, LANES)])
             block = jnp.concatenate(rows, axis=0)
             xt_ref[v, j * LANES : (j + 1) * LANES, :] = block.T
     a, b, c = split3(jnp.concatenate([xt_ref[v] for v in range(z.nv)], axis=1))
@@ -203,17 +197,35 @@
                     value = jnp.minimum(jnp.maximum(column[a], lowest), highest)
                     r = a * SIDE + b
                     both[r] = value if both[r] is None else both[r] + value
-        for r in range(REFS):
-            sums_ref[r * z.tracers + j * z.tpt : r * z.tracers + (j + 1) * z.tpt, :] = both[r]
-
-
-def serve_kernel(z, wown_ref, infar_ref, innear_ref, sums_ref, parts_ref, mass_ref, tofar_ref, tonear_ref, weight_ref):
-    weight_ref[...] = wown_ref[...] + infar_ref[0:REFS, :] + innear_ref[0:REFS, :]
+        low = lax.broadcasted_iota(jnp.int32, (1, LANES), 1) < z.elems
+        for r in range(z.wrows):
+            one, two = both[r], both[r + z.wrows]
+            folded = jnp.where(low, one, two) + pltpu.roll(jnp.where(low, two, one), z.elems, 1)
+            sums_ref[r * z.tracers + j * z.tpt : r * z.tracers + (j + 1) * z.tpt, :] = folded
+
+
+def serve_kernel(
+    z, wown_ref, infar_ref, innear_ref, sums_ref, parts_ref, spread_hbm, tofar_ref, tonear_ref, weight_ref, mass_ref, sem
+):
+    weight_ref[...] = wown_ref[...] + infar_ref[0 : z.wrows, :] + innear_ref[0 : z.wrows, :]
+    total = [None] * z.tiles
+    for r in range(z.wrows):
+        w = weight_ref[pl.ds(r, 1), :]
+        for j in range(z.tiles):
+            lo = r * z.tracers + j * z.tpt
+            term = sums_ref[lo : lo + z.tpt, :] * w
+            total[j] = term if total[j] is None else total[j] + term
+    total = jnp.concatenate(total, axis=0)
+    ones = jnp.ones((SUB, LANES), jnp.bfloat16)
+    mass = sum(mm_nt(ones, part) for part in split3(total))[0:1, :]
+    mass_ref[...] = jnp.broadcast_to(mass[None], mass_ref.shape)
+    copy = pltpu.make_async_copy(mass_ref, spread_hbm, sem)
+    copy.start()
     lane = lax.broadcasted_iota(jnp.int32, (1, LANES), 1)
     level = (lane // z.slots) % z.levels
     codes = []
     for ref in (infar_ref, innear_ref):
-        wanted = ref[REFS : REFS + 1, :].astype(jnp.int32)
+        wanted = ref[z.wrows : z.wrows + 1, :].astype(jnp.int32)
         codes.append(jnp.where(wanted >= 0, level * z.elems + wanted, -1))
     code = jnp.concatenate(codes, axis=1)
     row = lax.broadcasted_iota(jnp.int32, (z.cols, 2 * LANES), 0)
@@ -225,18 +237,7 @@
         for h in range(1, z.halves):
             value = jnp.where(half == h, rows[h * z.part : (h + 1) * z.part, at], value)
         ref[...] = value
-    total = [None] * z.tiles
-    for r in range(REFS):
-        w = weight_ref[pl.ds(r, 1), :]
-        for j in range(z.tiles):
-            lo = r * z.tracers + j * z.tpt
-            term = sums_ref[lo : lo + z.tpt, :] * w
-            total[j] = term if total[j] is None else total[j] + term
-    total = jnp.concatenate(total, axis=0)
-    ones = jnp.ones((SUB, LANES), jnp.bfloat16)
-    parts = split3(total)
-    mass = sum(mm_nt(ones, part) for part in parts)[0:1, :]
-    mass_ref[...] = jnp.broadcast_to(mass[None], mass_ref.shape)
+    copy.wait()
 
 
 def final_kernel(z, own_ref, far_ref, near_ref, codes_ref, coef_ref, out_ref, got_ref, turn_ref, flat_ref, sem):
@@ -284,12 +285,12 @@
     return pltpu.with_memory_space_constraint(x, pltpu.HBM)
 
 
-def call(kernel, z, outs, ins, args, scratch=(), flops=0, nbytes=0, limit=16):
+def call(kernel, z, outs, ins, args, scratch=(), flops=0, nbytes=0, limit=16, spaces=None):
     return pl.pallas_call(
         functools.partial(kernel, z),
         out_shape=[jax.ShapeDtypeStruct(shape, dtype) for shape, dtype in outs],
         in_specs=[pl.BlockSpec(memory_space=space) for space in ins],
-        out_specs=[pl.BlockSpec(memory_space=VMEM)] * len(outs),
+        out_specs=[pl.BlockSpec(memory_space=space) for space in spaces or [VMEM] * len(outs)],
         scratch_shapes=list(scratch),
         cost_estimate=pl.CostEstimate(flops=flops, bytes_accessed=nbytes, transcendentals=0),
         compiler_params=pltpu.CompilerParams(vmem_limit_bytes=limit << 20),
@@ -299,17 +300,17 @@
 def per_device(tracers, ref_index, requests, source, target_mean):
     elems, levels, width = tracers.shape
     z = Sizes(elems, levels, width, requests.shape[2])
-    assert z.per * elems == LANES and z.nv * z.per == levels and z.tiles * LANES == width
+    assert z.per == 2 and z.per * elems == LANES and z.nv * z.per == levels and z.tiles * LANES == width
     assert z.halves * levels * z.slots == LANES and z.part * z.halves == width
     f32, bf16, i32 = jnp.float32, jnp.bfloat16, jnp.int32
     flat = ((z.tiles, elems * levels, LANES), f32)
-    wown, ask_far, ask_near, raw, refs, own_source = call(
+    wown, ask_far, ask_near, refs, own_source = call(
         plan_kernel, z,
-        [((REFS, LANES), f32), ((REFS + SUB, LANES), f32), ((REFS + SUB, LANES), f32), flat,
+        [((z.wrows, LANES), f32), ((z.wrows + SUB, LANES), f32), ((z.wrows + SUB, LANES), f32),
          ((NPTS, elems), i32), ((1, elems), i32)],
-        (pltpu.HBM,) * 4, [in_hbm(a) for a in (tracers, requests, ref_index.T, source.reshape(1, elems))],
-        [SMEM(requests.shape, i32), pltpu.SemaphoreType.DMA((3,)), pltpu.SemaphoreType.DMA((z.tiles,))],
-        flops=10**6, nbytes=10**5,
+        (pltpu.HBM,) * 3, [in_hbm(a) for a in (requests, ref_index.T, source.reshape(1, elems))],
+        [SMEM(requests.shape, i32), pltpu.SemaphoreType.DMA((3,))],
+        flops=10**9, nbytes=10**7,
     )
     count = lax.axis_size("elem")
     assert count % 2 == 0
@@ -319,15 +320,19 @@
     in_near = lax.ppermute(ask_near, "elem", near)
     parts, own, sums, codes, coef = call(
         prep_kernel, z,
-        [((3, width, z.cols), bf16), ((width, z.cols), f32), ((REFS * z.tracers, LANES), f32), ((SUB, z.cols), i32),
+        [((3, width, z.cols), bf16), ((width, z.cols), f32), ((z.wrows * z.tracers, LANES), f32), ((SUB, z.cols), i32),
          ((NPTS * NPTS, LANES), f32)],
-        (VMEM,) * 3, (raw, refs, own_source), [VMEM((z.nv, width, LANES), f32)], flops=10**8, nbytes=4 * 10**6,
+        (VMEM, VMEM, VMEM), (tracers, refs, own_source),
+        [VMEM((z.nv, width, LANES), f32)], flops=10**8, nbytes=4 * 10**6,
     )
     axes = ("elem", "lev")
+    spread_shape = ((lax.axis_size(axes), 1, z.tracers), f32)
     spread, to_far, to_near = call(
         serve_kernel, z,
-        [((lax.axis_size(axes), 1, z.tracers), f32), ((z.part, LANES), f32), ((z.part, LANES), f32)],
-        (VMEM,) * 5, (wown, in_far, in_near, sums, parts), [VMEM((REFS, LANES), f32)], flops=10**7, nbytes=3 * 10**6,
+        [spread_shape, ((z.part, LANES), f32), ((z.part, LANES), f32)],
+        (VMEM,) * 5, (wown, in_far, in_near, sums, parts),
+        [VMEM((z.wrows, LANES), f32), VMEM(*spread_shape), pltpu.SemaphoreType.DMA(())],
+        flops=10**7, nbytes=3 * 10**6, spaces=(pltpu.HBM, VMEM, VMEM),
     )
     from_far = lax.ppermute(to_far, "elem", far)
     from_near = lax.ppermute(to_near, "elem", near)

time: 25.7 us -> 25.1 us (0.977)
  waiting for transfers between devices: 4.71 us -> 4.39 us
  starting transfers between devices: 13.7 us -> 13.4 us
    ppermute x1, waiting for transfers between devices: 0.31 us -> 0.01 us  [per_device(): in_far = lax.ppermute(ask_far, 'elem', far)]
    all_to_all x1, starting transfers between devices: 5.68 us -> 5.4 us  [per_device(): every = lax.all_to_all(spread, axes, 0, 0)]
  transfers between devices with their start and end apart: 5 -> 5, of which waited for: 3 -> 2; matrix products, arithmetic and copies ran while one was open for 1% -> 1% of each run, Pallas kernels for 6% -> 7%
where the time goes in v4:
time: 25.1 us; the launch traced here: 24.9 us
  starting transfers between devices  13.4 us (53%)
  Pallas kernels  5.92 us (24%)
  waiting for transfers between devices  4.39 us (17%)
  other arithmetic  1.01 us (4%)
    pallas_call x4, Pallas kernels, call(): pl.pallas_call(functools.partial(kernel, z), out_shape=[jax.ShapeDtypeStr...  5.92 us
    all_to_all x1, starting transfers between devices, per_device(): every = lax.all_to_all(spread, axes, 0, 0)  5.4 us
    ppermute x1, starting transfers between devices, per_device(): in_far = lax.ppermute(ask_far, 'elem', far)  4.58 us
    all_to_all x1, waiting for transfers between devices, per_device(): every = lax.all_to_all(spread, axes, 0, 0)  3.81 us
    ppermute x1, starting transfers between devices, per_device(): from_far = lax.ppermute(to_far, 'elem', far)  3.41 us
    mul x1, other arithmetic, per_device(): return shaped * jnp.repeat(factor, NPTS)[None, None, :]  0.95 us
    ppermute x1, waiting for transfers between devices, per_device(): from_far = lax.ppermute(to_far, 'elem', far)  0.58 us
  transfers between devices with their start and end apart: 5, of which 2 were waited for; matrix products, arithmetic and copies ran while one was open for 1% of the time, Pallas kernels for 7%

profile of v4, /device:TPU:0, one launch (start us, length us, event | category | flops | bytes accessed | tf_op | source)
XLA Modules:
  0.0 24.9 jit_solution(14120611716106302078)
XLA Ops:
  0.0 0.0 copy-start
  0.0 1.1 %shard_map.55 = (f32[32,128]{1,0:T(8,128)S(1)}, f32[40,128]{1,0:T(8,128)S(1)}, f32[40,128]{1,0:T(8,128)S(1)}, s32[16,64]{1,0:T(8,128)S(1)}, s32[1,64]{1,0:T(1,128)S(1)}) custom-call(s32[1,2,16]{2,1,0:T(2,128)} %req_hbm.1, s32[16,64]{1,0:T(8,128)} %bitcast.2, s32[1,64]{1,0:T(1,128)} %bitcast.3), custom_call_target="tpu_custom_call" | custom-call | flops 1000000000 | bytes 10000000 | tf_op jit(solution)/shard_map/pallas_call | solution.py:289
  1.1 4.6 %collective-permute-start = (f32[40,128]{1,0:T(8,128)S(1)}, f32[40,128]{1,0:T(8,128)S(1)}, u32[]{:S(2)}, u32[]{:S(2)}) collective-permute-start(f32[40,128]{1,0:T(8,128)S(1)} %get-tuple-element.22), channel_id=1, source_target_pairs={{0,28},{4,8},{8,4},{12,16},{16,12},{20,24},{24,20},{28,0},{1,29},{... | collective-permute-start | bytes 61448 | tf_op jit(solution)/shard_map/ppermute | solution.py:319
  5.7 0.0 collective-permute-start.1
  5.7 0.0 copy-done
  5.7 1.8 %shard_map.56 = (bf16[3,640,256]{2,1,0:T(8,128)(2,1)S(1)}, f32[640,256]{1,0:T(8,128)S(1)}, f32[1280,128]{1,0:T(8,128)S(1)}, s32[8,256]{1,0:T(8,128)S(1)}, f32[256,128]{1,0:T(8,128)S(1)}) custom-call(f32[64,4,640]{2,1,0:T(4,128)S(1)} %copy-done, s32[16,64]{1,0:T(8,128)S(1)} %get-tuple-element.18.ref_ref, s32[1,64]{1,0:T(1,128)S(1)} %get-tuple-element.19.src_ref), custom_call_target="tpu_custom_call" | custom-call | flops 100000000 | bytes 4000000 | tf_op jit(solution)/shard_map/pallas_call | solution.py:289
  7.6 0.0 collective-permute-done.infar_ref
  7.6 0.0 collective-permute-done.1.innear_ref
  7.6 0.9 %shard_map.57 = (f32[32,1,40]{2,1,0:T(1,128)}, f32[320,128]{1,0:T(8,128)S(1)}, f32[320,128]{1,0:T(8,128)S(1)}) custom-call(f32[32,128]{1,0:T(8,128)S(1)} %get-tuple-element.21.wown_ref, f32[40,128]{1,0:T(8,128)S(1)} %collective-permute-done.infar_ref, f32[40,128]{1,0:T(8,128)S(1)} %collective-permute-done.1.innear_ref, ...), custom_call_target="tpu_custom_call" | custom-call | flops 10000000 | bytes 3000000 | tf_op jit(solution)/shard_map/pallas_call | solution.py:289
  8.5 5.4 %all-to-all-start = ((f32[32,1,40]{2,1,0:T(1,128)}), f32[32,1,40]{2,1,0:T(1,128)S(1)}, u32[]{:S(2)}, u32[]{:S(2)}) async-start(f32[32,1,40]{2,1,0:T(1,128)} %get-tuple-element.30), calls=%async_computation | async-start | bytes 32768 | tf_op jit(solution)/shard_map/all_to_all | solution.py:339
  13.9 3.4 %collective-permute-start.2 = (f32[320,128]{1,0:T(8,128)S(1)}, f32[320,128]{1,0:T(8,128)S(1)}, u32[]{:S(2)}, u32[]{:S(2)}) collective-permute-start(f32[320,128]{1,0:T(8,128)S(1)} %get-tuple-element.26), channel_id=1, source_target_pairs={{0,28},{4,8},{8,4},{12,16},{16,12},{20,24},{24,20},{28,0},{1,29},{... | collective-permute-start | bytes 491528 | tf_op jit(solution)/shard_map/ppermute | solution.py:337
  17.3 0.0 copy-start.1
  17.3 0.0 collective-permute-start.3
  17.3 3.8 %all-to-all-done = f32[32,1,40]{2,1,0:T(1,128)S(1)} async-done(((f32[32,1,40]{2,1,0:T(1,128)}), f32[32,1,40]{2,1,0:T(1,128)S(1)}, u32[]{:S(2)}, u32[]{:S(2)}) %all-to-all-start) | async-done | bytes 5152 | tf_op jit(solution)/shard_map/all_to_all | solution.py:339
  21.1 0.1 reduce_sum.9
  21.2 0.0 copy-done.1
  21.2 0.1 broadcast_in_dim.3
  21.2 0.1 mul.18
  21.3 0.6 %collective-permute-done.2.far_ref = f32[320,128]{1,0:T(8,128)S(1)} collective-permute-done((f32[320,128]{1,0:T(8,128)S(1)}, f32[320,128]{1,0:T(8,128)S(1)}, u32[]{:S(2)}, u32[]{:S(2)}) %collective-permute-start.2) | collective-permute-done | bytes 163872 | tf_op jit(solution)/shard_map/ppermute | solution.py:337
  21.9 0.0 collective-permute-done.3.near_ref
  21.9 2.1 %shard_map.58 = f32[64,4,640]{2,1,0:T(4,128)S(1)} custom-call(f32[640,256]{1,0:T(8,128)S(1)} %get-tuple-element.20.own_ref, f32[320,128]{1,0:T(8,128)S(1)} %collective-permute-done.2.far_ref, f32[320,128]{1,0:T(8,128)S(1)} %collective-permute-done.3.near_ref, s32[8,256]{1,0:T(8,128)S(1)} %get-tuple-element.28.codes_ref, ...), custom_call_target="tpu_custom_call" | custom-call | flops 100000000 | bytes 3000000 | tf_op jit(solution)/shard_map/pallas_call | solution.py:289
  24.0 1.0 %broadcast_multiply_fusion = f32[64,4,640]{2,1,0:T(4,128)} fusion(f32[64,4,640]{2,1,0:T(4,128)S(1)} %shard_map.58, f32[640]{0:T(1024)S(1)} %mul.18), kind=kLoop, calls=%fused_computation | loop fusion | flops 163840 | bytes 1313280 | tf_op jit(solution)/shard_map/mul | solution.py:350
  (1 shorter events, 0.0 us)
Async XLA Ops:
  0.0 5.7 %copy-start = (f32[64,4,640]{2,1,0:T(4,128)S(1)}, f32[64,4,640]{2,1,0:T(4,128)}, u32[]{:S(2)}) copy-start(f32[64,4,640]{2,1,0:T(4,128)} %x_ref.1) | copy-start | bytes 1966084
  1.1 6.4 %collective-permute-start = (f32[40,128]{1,0:T(8,128)S(1)}, f32[40,128]{1,0:T(8,128)S(1)}, u32[]{:S(2)}, u32[]{:S(2)}) collective-permute-start(f32[40,128]{1,0:T(8,128)S(1)} %get-tuple-element.22), channel_id=1, source_target_pairs={{0,28},{4,8},{8,4},{12,16},{16,12},{20,24},{24,20},{28,0},{1,29},{... | collective-permute-start | bytes 61448 | tf_op jit(solution)/shard_map/ppermute | solution.py:319
  5.7 1.9 %collective-permute-start.1 = (f32[40,128]{1,0:T(8,128)S(1)}, f32[40,128]{1,0:T(8,128)S(1)}, u32[]{:S(2)}, u32[]{:S(2)}) collective-permute-start(f32[40,128]{1,0:T(8,128)S(1)} %get-tuple-element.23), channel_id=1, source_target_pairs={{0,4},{4,0},{8,12},{12,8},{16,20},{20,16},{24,28},{28,24},{1,5},{5... | collective-permute-start | bytes 61448 | tf_op jit(solution)/shard_map/ppermute | solution.py:320
  8.5 12.6 %all-to-all-start = ((f32[32,1,40]{2,1,0:T(1,128)}), f32[32,1,40]{2,1,0:T(1,128)S(1)}, u32[]{:S(2)}, u32[]{:S(2)}) async-start(f32[32,1,40]{2,1,0:T(1,128)} %get-tuple-element.30), calls=%async_computation | async-start | bytes 32768 | tf_op jit(solution)/shard_map/all_to_all | solution.py:339
  13.9 8.0 %collective-permute-start.2 = (f32[320,128]{1,0:T(8,128)S(1)}, f32[320,128]{1,0:T(8,128)S(1)}, u32[]{:S(2)}, u32[]{:S(2)}) collective-permute-start(f32[320,128]{1,0:T(8,128)S(1)} %get-tuple-element.26), channel_id=1, source_target_pairs={{0,28},{4,8},{8,4},{12,16},{16,12},{20,24},{24,20},{28,0},{1,29},{... | collective-permute-start | bytes 491528 | tf_op jit(solution)/shard_map/ppermute | solution.py:337
  17.3 3.9 %copy-start.1 = (f32[40]{0:T(128)S(1)}, f32[40]{0:T(128)}, u32[]{:S(2)}) copy-start(f32[40]{0:T(128)} %param.9) | copy-start | bytes 484
  17.3 4.6 %collective-permute-start.3 = (f32[320,128]{1,0:T(8,128)S(1)}, f32[320,128]{1,0:T(8,128)S(1)}, u32[]{:S(2)}, u32[]{:S(2)}) collective-permute-start(f32[320,128]{1,0:T(8,128)S(1)} %get-tuple-element.27), channel_id=1, source_target_pairs={{0,4},{4,0},{8,12},{12,8},{16,20},{20,16},{24,28},{28,24},{1,5},{5... | collective-permute-start | bytes 491528 | tf_op jit(solution)/shard_map/ppermute | solution.py:338

commit v5 on v4

--- a/solution.py
+++ b/solution.py
@@ -240,7 +240,7 @@
     copy.wait()
 
 
-def final_kernel(z, own_ref, far_ref, near_ref, codes_ref, coef_ref, out_ref, got_ref, turn_ref, flat_ref, sem):
+def final_kernel(z, own_ref, far_ref, near_ref, codes_ref, coef_ref, flat_ref, got_ref, turn_ref):
     halo = jnp.concatenate([far_ref[...], near_ref[...]], axis=1)
     parts = split3(halo)
     row = lax.broadcasted_iota(jnp.int32, (2 * LANES, z.cols), 0)
@@ -250,7 +250,6 @@
         got = own_ref[at, :] + onehot_dot(parts, pick)
         for v in range(z.nv):
             got_ref[v, at, :] = got[:, v * LANES : (v + 1) * LANES]
-    copies = []
     for j in range(z.tiles):
         xs, low, high = [], [], []
         for v in range(z.nv):
@@ -271,9 +270,21 @@
                 for e in range(0, z.elems, SUB):
                     piece = block[q * z.elems + e : q * z.elems + e + SUB, :]
                     flat_ref[j, pl.ds(e * z.levels + level, SUB, stride=z.levels), :] = piece
+
+
+def scale_kernel(z, whole_weight, every_ref, mean_ref, flat_ref, out_hbm, stage_ref, sem):
+    total = tree(jnp.add, [every_ref[m] for m in range(every_ref.shape[0])])
+    factor = mean_ref[...] * whole_weight / total
+    factor = jnp.concatenate([factor, jnp.zeros((1, LANES - z.tracers), jnp.float32)], axis=1)
+    factor = jnp.broadcast_to(factor, (SUB, LANES))
+    lane = lax.broadcasted_iota(jnp.int32, (SUB, LANES), 1)
+    copies = []
+    for j in range(z.tiles):
+        mine = jnp.take_along_axis(factor, j * z.tpt + lane // NPTS, axis=1)
+        stage_ref[j] = flat_ref[j] * mine[0:1, :]
         copies.append(
             pltpu.make_async_copy(
-                flat_ref.at[j].reshape(z.elems, z.levels, LANES), out_ref.at[:, :, pl.ds(j * LANES, LANES)], sem.at[j]
+                stage_ref.at[j].reshape(z.elems, z.levels, LANES), out_hbm.at[:, :, pl.ds(j * LANES, LANES)], sem.at[j]
             )
         )
         copies[-1].start()
@@ -339,15 +350,19 @@
     every = lax.all_to_all(spread, axes, 0, 0)
     (shaped,) = call(
         final_kernel, z,
+        [flat],
+        (VMEM,) * 5, (own, from_far, from_near, codes, coef),
+        [VMEM((z.nv, width, LANES), f32), VMEM((z.nv, LANES, LANES), f32)],
+        flops=10**8, nbytes=3 * 10**6,
+    )
+    whole_weight = 36.0 * 4.0 * elems * count * levels * lax.axis_size("lev")
+    (out,) = call(
+        lambda z, *refs: scale_kernel(z, whole_weight, *refs), z,
         [((elems, levels, width), f32)],
-        (VMEM,) * 5, (own, from_far, from_near, codes, coef),
-        [VMEM((z.nv, width, LANES), f32), VMEM((z.nv, LANES, LANES), f32), VMEM(*flat), pltpu.SemaphoreType.DMA((z.tiles,))],
-        flops=10**8, nbytes=3 * 10**6,
-    )
-    global_mass = every.sum(axis=(0, 1))
-    whole_weight = 36.0 * 4.0 * elems * count * levels * lax.axis_size("lev")
-    factor = target_mean * whole_weight / global_mass
-    return shaped * jnp.repeat(factor, NPTS)[None, None, :]
+        (VMEM,) * 3, (every, target_mean.reshape(1, z.tracers), shaped),
+        [VMEM(*flat), pltpu.SemaphoreType.DMA((z.tiles,))], flops=10**6, nbytes=10**6, spaces=(pltpu.HBM,),
+    )
+    return out
 
 
 def solution(mesh):

time: 25.1 us -> 23.1 us (0.920)
  starting transfers between devices: 13.4 us -> 10.9 us
  waiting for transfers between devices: 4.39 us -> 5.54 us
  other arithmetic: 1.01 us -> 0 us
  Pallas kernels: 5.92 us -> 6.39 us
    all_to_all x1, starting transfers between devices: 5.4 us -> 3.14 us  [per_device(): every = lax.all_to_all(spread, axes, 0, 0)]
    mul x1 -> x0, other arithmetic: 0.95 us -> none  [per_device(): return shaped * jnp.repeat(factor, NPTS)[None, None, :]]
    all_to_all x1, waiting for transfers between devices: 3.81 us -> 4.47 us  [per_device(): every = lax.all_to_all(spread, axes, 0, 0)]
    ppermute x1, waiting for transfers between devices: 0.58 us -> 1.06 us  [per_device(): from_far = lax.ppermute(to_far, 'elem', far)]
    pallas_call x4 -> x5, Pallas kernels: 5.92 us -> 6.39 us  [call(): pl.pallas_call(functools.partial(kernel, z), out_shape=[jax.ShapeDtypeStr...]
  transfers between devices with their start and end apart: 5 -> 5, of which waited for: 2 -> 2; matrix products, arithmetic and copies ran while one was open for 1% -> 0% of each run, Pallas kernels for 7% -> 15%
where the time goes in v5:
time: 23.1 us; the launch traced here: 22.9 us
  starting transfers between devices  10.9 us (47%)
  Pallas kernels  6.39 us (28%)
  waiting for transfers between devices  5.54 us (24%)
    pallas_call x5, Pallas kernels, call(): pl.pallas_call(functools.partial(kernel, z), out_shape=[jax.ShapeDtypeStr...  6.39 us
    ppermute x1, starting transfers between devices, per_device(): in_far = lax.ppermute(ask_far, 'elem', far)  4.58 us
    all_to_all x1, waiting for transfers between devices, per_device(): every = lax.all_to_all(spread, axes, 0, 0)  4.47 us
    ppermute x1, starting transfers between devices, per_device(): from_far = lax.ppermute(to_far, 'elem', far)  3.21 us
    all_to_all x1, starting transfers between devices, per_device(): every = lax.all_to_all(spread, axes, 0, 0)  3.14 us
    ppermute x1, waiting for transfers between devices, per_device(): from_far = lax.ppermute(to_far, 'elem', far)  1.06 us
  transfers between devices with their start and end apart: 5, of which 2 were waited for; matrix products, arithmetic and copies ran while one was open for 0% of the time, Pallas kernels for 15%

profile of v5, /device:TPU:0, one launch (start us, length us, event | category | flops | bytes accessed | tf_op | source)
XLA Modules:
  0.0 22.9 jit_solution(10213356664056909809)
XLA Ops:
  0.0 0.0 copy-start
  0.0 1.1 %shard_map.55 = (f32[32,128]{1,0:T(8,128)S(1)}, f32[40,128]{1,0:T(8,128)S(1)}, f32[40,128]{1,0:T(8,128)S(1)}, s32[16,64]{1,0:T(8,128)S(1)}, s32[1,64]{1,0:T(1,128)S(1)}) custom-call(s32[1,2,16]{2,1,0:T(2,128)} %req_hbm.1, s32[16,64]{1,0:T(8,128)} %bitcast.4, s32[1,64]{1,0:T(1,128)} %bitcast.5), custom_call_target="tpu_custom_call" | custom-call | flops 1000000000 | bytes 10000000 | tf_op jit(solution)/shard_map/pallas_call | solution.py:300
  1.1 4.6 %collective-permute-start = (f32[40,128]{1,0:T(8,128)S(1)}, f32[40,128]{1,0:T(8,128)S(1)}, u32[]{:S(2)}, u32[]{:S(2)}) collective-permute-start(f32[40,128]{1,0:T(8,128)S(1)} %get-tuple-element.19), channel_id=1, source_target_pairs={{0,28},{4,8},{8,4},{12,16},{16,12},{20,24},{24,20},{28,0},{1,29},{... | collective-permute-start | bytes 61448 | tf_op jit(solution)/shard_map/ppermute | solution.py:330
  5.7 0.0 collective-permute-start.1
  5.7 0.0 copy-done
  5.7 1.8 %shard_map.56 = (bf16[3,640,256]{2,1,0:T(8,128)(2,1)S(1)}, f32[640,256]{1,0:T(8,128)S(1)}, f32[1280,128]{1,0:T(8,128)S(1)}, s32[8,256]{1,0:T(8,128)S(1)}, f32[256,128]{1,0:T(8,128)S(1)}) custom-call(f32[64,4,640]{2,1,0:T(4,128)S(1)} %copy-done, s32[16,64]{1,0:T(8,128)S(1)} %get-tuple-element.21.ref_ref, s32[1,64]{1,0:T(1,128)S(1)} %get-tuple-element.22.src_ref), custom_call_target="tpu_custom_call" | custom-call | flops 100000000 | bytes 4000000 | tf_op jit(solution)/shard_map/pallas_call | solution.py:300
  7.6 0.0 collective-permute-done.infar_ref
  7.6 0.0 collective-permute-done.1.innear_ref
  7.6 0.9 %shard_map.57 = (f32[32,1,40]{2,1,0:T(1,128)}, f32[320,128]{1,0:T(8,128)S(1)}, f32[320,128]{1,0:T(8,128)S(1)}) custom-call(f32[32,128]{1,0:T(8,128)S(1)} %get-tuple-element.18.wown_ref, f32[40,128]{1,0:T(8,128)S(1)} %collective-permute-done.infar_ref, f32[40,128]{1,0:T(8,128)S(1)} %collective-permute-done.1.innear_ref, ...), custom_call_target="tpu_custom_call" | custom-call | flops 10000000 | bytes 3000000 | tf_op jit(solution)/shard_map/pallas_call | solution.py:300
  8.5 3.2 %collective-permute-start.2 = (f32[320,128]{1,0:T(8,128)S(1)}, f32[320,128]{1,0:T(8,128)S(1)}, u32[]{:S(2)}, u32[]{:S(2)}) collective-permute-start(f32[320,128]{1,0:T(8,128)S(1)} %get-tuple-element.27), channel_id=1, source_target_pairs={{0,28},{4,8},{8,4},{12,16},{16,12},{20,24},{24,20},{28,0},{1,29},{... | collective-permute-start | bytes 491528 | tf_op jit(solution)/shard_map/ppermute | solution.py:348
  11.7 0.0 collective-permute-start.3
  11.7 3.1 %all-to-all-start = ((f32[32,1,40]{2,1,0:T(1,128)}), f32[32,1,40]{2,1,0:T(1,128)S(1)}, u32[]{:S(2)}, u32[]{:S(2)}) async-start(f32[32,1,40]{2,1,0:T(1,128)} %get-tuple-element.25), calls=%async_computation | async-start | bytes 32768 | tf_op jit(solution)/shard_map/all_to_all | solution.py:350
  14.8 1.1 %collective-permute-done.2.far_ref = f32[320,128]{1,0:T(8,128)S(1)} collective-permute-done((f32[320,128]{1,0:T(8,128)S(1)}, f32[320,128]{1,0:T(8,128)S(1)}, u32[]{:S(2)}, u32[]{:S(2)}) %collective-permute-start.2) | collective-permute-done | bytes 163872 | tf_op jit(solution)/shard_map/ppermute | solution.py:348
  15.9 0.0 collective-permute-done.3.near_ref
  15.9 1.6 %shard_map.58.refs_2_ = f32[5,256,128]{2,1,0:T(8,128)S(1)} custom-call(f32[640,256]{1,0:T(8,128)S(1)} %get-tuple-element.26.own_ref, f32[320,128]{1,0:T(8,128)S(1)} %collective-permute-done.2.far_ref, f32[320,128]{1,0:T(8,128)S(1)} %collective-permute-done.3.near_ref, s32[8,256]{1,0:T(8,128)S(1)} %get-tuple-element.29.codes_ref, ...), custom_call_target="tpu_custom_call" | custom-call | flops 100000000 | bytes 3000000 | tf_op jit(solution)/shard_map/pallas_call | solution.py:300
  17.5 0.0 copy-start.1
  17.5 4.5 %all-to-all-done.refs_0_ = f32[32,1,40]{2,1,0:T(1,128)S(1)} async-done(((f32[32,1,40]{2,1,0:T(1,128)}), f32[32,1,40]{2,1,0:T(1,128)S(1)}, u32[]{:S(2)}, u32[]{:S(2)}) %all-to-all-start) | async-done | bytes 5152 | tf_op jit(solution)/shard_map/all_to_all | solution.py:350
  22.0 0.0 copy-done.1
  22.0 1.0 %shard_map.59 = f32[64,4,640]{2,1,0:T(4,128)} custom-call(f32[32,1,40]{2,1,0:T(1,128)S(1)} %all-to-all-done.refs_0_, f32[1,40]{1,0:T(1,128)S(1)} %bitcast.3, f32[5,256,128]{2,1,0:T(8,128)S(1)} %shard_map.58.refs_2_), custom_call_target="tpu_custom_call" | custom-call | flops 1000000 | bytes 1000000 | tf_op jit(solution)/shard_map/pallas_call | solution.py:300
Async XLA Ops:
  0.0 5.7 %copy-start = (f32[64,4,640]{2,1,0:T(4,128)S(1)}, f32[64,4,640]{2,1,0:T(4,128)}, u32[]{:S(2)}) copy-start(f32[64,4,640]{2,1,0:T(4,128)} %x_ref.1) | copy-start | bytes 1966084
  1.1 6.4 %collective-permute-start = (f32[40,128]{1,0:T(8,128)S(1)}, f32[40,128]{1,0:T(8,128)S(1)}, u32[]{:S(2)}, u32[]{:S(2)}) collective-permute-start(f32[40,128]{1,0:T(8,128)S(1)} %get-tuple-element.19), channel_id=1, source_target_pairs={{0,28},{4,8},{8,4},{12,16},{16,12},{20,24},{24,20},{28,0},{1,29},{... | collective-permute-start | bytes 61448 | tf_op jit(solution)/shard_map/ppermute | solution.py:330
  5.7 1.9 %collective-permute-start.1 = (f32[40,128]{1,0:T(8,128)S(1)}, f32[40,128]{1,0:T(8,128)S(1)}, u32[]{:S(2)}, u32[]{:S(2)}) collective-permute-start(f32[40,128]{1,0:T(8,128)S(1)} %get-tuple-element.20), channel_id=1, source_target_pairs={{0,4},{4,0},{8,12},{12,8},{16,20},{20,16},{24,28},{28,24},{1,5},{5... | collective-permute-start | bytes 61448 | tf_op jit(solution)/shard_map/ppermute | solution.py:331
  8.5 7.4 %collective-permute-start.2 = (f32[320,128]{1,0:T(8,128)S(1)}, f32[320,128]{1,0:T(8,128)S(1)}, u32[]{:S(2)}, u32[]{:S(2)}) collective-permute-start(f32[320,128]{1,0:T(8,128)S(1)} %get-tuple-element.27), channel_id=1, source_target_pairs={{0,28},{4,8},{8,4},{12,16},{16,12},{20,24},{24,20},{28,0},{1,29},{... | collective-permute-start | bytes 491528 | tf_op jit(solution)/shard_map/ppermute | solution.py:348
  11.7 4.2 %collective-permute-start.3 = (f32[320,128]{1,0:T(8,128)S(1)}, f32[320,128]{1,0:T(8,128)S(1)}, u32[]{:S(2)}, u32[]{:S(2)}) collective-permute-start(f32[320,128]{1,0:T(8,128)S(1)} %get-tuple-element.28), channel_id=1, source_target_pairs={{0,4},{4,0},{8,12},{12,8},{16,20},{20,16},{24,28},{28,24},{1,5},{5... | collective-permute-start | bytes 491528 | tf_op jit(solution)/shard_map/ppermute | solution.py:349
  11.7 10.3 %all-to-all-start = ((f32[32,1,40]{2,1,0:T(1,128)}), f32[32,1,40]{2,1,0:T(1,128)S(1)}, u32[]{:S(2)}, u32[]{:S(2)}) async-start(f32[32,1,40]{2,1,0:T(1,128)} %get-tuple-element.25), calls=%async_computation | async-start | bytes 32768 | tf_op jit(solution)/shard_map/all_to_all | solution.py:350
  17.5 4.5 %copy-start.1 = (f32[40]{0:T(128)S(1)}, f32[40]{0:T(128)}, u32[]{:S(2)}) copy-start(f32[40]{0:T(128)} %param.9) | copy-start | bytes 484

commit v6 on v5

--- a/solution.py
+++ b/solution.py
@@ -169,8 +169,7 @@
     return values[0]
 
 
-def prep_kernel(z, x_ref, ref_ref, src_ref, parts_ref, own_ref, sums_ref, codes_ref, coef_ref, xt_ref):
-    tables(z, src_ref[...], ref_ref[...], codes_ref, coef_ref)
+def prep_kernel(z, x_ref, parts_ref, sums_ref, xt_ref):
     for j in range(z.tiles):
         for v in range(z.nv):
             rows = []
@@ -182,9 +181,6 @@
             xt_ref[v, j * LANES : (j + 1) * LANES, :] = block.T
     a, b, c = split3(jnp.concatenate([xt_ref[v] for v in range(z.nv)], axis=1))
     parts_ref[0], parts_ref[1], parts_ref[2] = a, b, c
-    row = lax.broadcasted_iota(jnp.int32, (z.cols, z.cols), 0)
-    pick = (row == codes_ref[0:1, :]).astype(jnp.float32).astype(jnp.bfloat16)
-    own_ref[...] = onehot_dot((a, b, c), pick)
     for j in range(z.tiles):
         both = [None] * REFS
         for v in range(z.nv):
@@ -208,46 +204,58 @@
     z, wown_ref, infar_ref, innear_ref, sums_ref, parts_ref, spread_hbm, tofar_ref, tonear_ref, weight_ref, mass_ref, sem
 ):
     weight_ref[...] = wown_ref[...] + infar_ref[0 : z.wrows, :] + innear_ref[0 : z.wrows, :]
-    total = [None] * z.tiles
+    terms = [[] for _ in range(z.tiles)]
     for r in range(z.wrows):
         w = weight_ref[pl.ds(r, 1), :]
         for j in range(z.tiles):
             lo = r * z.tracers + j * z.tpt
             term = sums_ref[lo : lo + z.tpt, :] * w
-            total[j] = term if total[j] is None else total[j] + term
-    total = jnp.concatenate(total, axis=0)
-    ones = jnp.ones((SUB, LANES), jnp.bfloat16)
-    mass = sum(mm_nt(ones, part) for part in split3(total))[0:1, :]
+            if len(terms[j]) < 4:
+                terms[j].append(term)
+            else:
+                terms[j][r % 4] = terms[j][r % 4] + term
+    total = jnp.concatenate([tree(jnp.add, parts) for parts in terms], axis=0)
+    mass = jnp.sum(total.T, axis=0, keepdims=True)
     mass_ref[...] = jnp.broadcast_to(mass[None], mass_ref.shape)
     copy = pltpu.make_async_copy(mass_ref, spread_hbm, sem)
     copy.start()
-    lane = lax.broadcasted_iota(jnp.int32, (1, LANES), 1)
-    level = (lane // z.slots) % z.levels
-    codes = []
-    for ref in (infar_ref, innear_ref):
-        wanted = ref[z.wrows : z.wrows + 1, :].astype(jnp.int32)
-        codes.append(jnp.where(wanted >= 0, level * z.elems + wanted, -1))
-    code = jnp.concatenate(codes, axis=1)
-    row = lax.broadcasted_iota(jnp.int32, (z.cols, 2 * LANES), 0)
-    pick = (row == code).astype(jnp.float32).astype(jnp.bfloat16)
-    rows = onehot_dot((parts_ref[0], parts_ref[1], parts_ref[2]), pick)
-    half = lane // (z.levels * z.slots)
-    for ref, at in ((tofar_ref, slice(0, LANES)), (tonear_ref, slice(LANES, 2 * LANES))):
-        value = rows[0 : z.part, at]
-        for h in range(1, z.halves):
-            value = jnp.where(half == h, rows[h * z.part : (h + 1) * z.part, at], value)
-        ref[...] = value
+
+    @pl.when(lax.axis_index("elem") >= 0)
+    def _():
+        lane = lax.broadcasted_iota(jnp.int32, (1, LANES), 1)
+        level = (lane // z.slots) % z.levels
+        codes = []
+        for ref in (infar_ref, innear_ref):
+            wanted = ref[z.wrows : z.wrows + 1, :].astype(jnp.int32)
+            codes.append(jnp.where(wanted >= 0, level * z.elems + wanted, -1))
+        code = jnp.concatenate(codes, axis=1)
+        row = lax.broadcasted_iota(jnp.int32, (z.cols, 2 * LANES), 0)
+        pick = (row == code).astype(jnp.float32).astype(jnp.bfloat16)
+        rows = onehot_dot((parts_ref[0], parts_ref[1], parts_ref[2]), pick)
+        half = lane // (z.levels * z.slots)
+        for ref, at in ((tofar_ref, slice(0, LANES)), (tonear_ref, slice(LANES, 2 * LANES))):
+            value = rows[0 : z.part, at]
+            for h in range(1, z.halves):
+                value = jnp.where(half == h, rows[h * z.part : (h + 1) * z.part, at], value)
+            ref[...] = value
+
     copy.wait()
 
 
-def final_kernel(z, own_ref, far_ref, near_ref, codes_ref, coef_ref, flat_ref, got_ref, turn_ref):
+def final_kernel(
+    z, parts_ref, far_ref, near_ref, ref_ref, src_ref, flat_ref, codes_ref, coef_ref, got_ref, turn_ref
+):
+    tables(z, src_ref[...], ref_ref[...], codes_ref, coef_ref)
+    row = lax.broadcasted_iota(jnp.int32, (z.cols, z.cols), 0)
+    pick = (row == codes_ref[0:1, :]).astype(jnp.float32).astype(jnp.bfloat16)
+    own = onehot_dot((parts_ref[0], parts_ref[1], parts_ref[2]), pick)
     halo = jnp.concatenate([far_ref[...], near_ref[...]], axis=1)
     parts = split3(halo)
     row = lax.broadcasted_iota(jnp.int32, (2 * LANES, z.cols), 0)
     for h in range(z.halves):
         pick = (row == codes_ref[1 + h : 2 + h, :]).astype(jnp.float32).astype(jnp.bfloat16)
         at = slice(h * z.part, (h + 1) * z.part)
-        got = own_ref[at, :] + onehot_dot(parts, pick)
+        got = own[at, :] + onehot_dot(parts, pick)
         for v in range(z.nv):
             got_ref[v, at, :] = got[:, v * LANES : (v + 1) * LANES]
     for j in range(z.tiles):
@@ -329,12 +337,10 @@
     near = [(i, i + 1 if i % 2 == 0 else i - 1) for i in range(count)]
     in_far = lax.ppermute(ask_far, "elem", far)
     in_near = lax.ppermute(ask_near, "elem", near)
-    parts, own, sums, codes, coef = call(
+    parts, sums = call(
         prep_kernel, z,
-        [((3, width, z.cols), bf16), ((width, z.cols), f32), ((z.wrows * z.tracers, LANES), f32), ((SUB, z.cols), i32),
-         ((NPTS * NPTS, LANES), f32)],
-        (VMEM, VMEM, VMEM), (tracers, refs, own_source),
-        [VMEM((z.nv, width, LANES), f32)], flops=10**8, nbytes=4 * 10**6,
+        [((3, width, z.cols), bf16), ((z.wrows * z.tracers, LANES), f32)],
+        (VMEM,), (tracers,), [VMEM((z.nv, width, LANES), f32)], flops=10**8, nbytes=4 * 10**6,
     )
     axes = ("elem", "lev")
     spread_shape = ((lax.axis_size(axes), 1, z.tracers), f32)
@@ -351,8 +357,8 @@
     (shaped,) = call(
         final_kernel, z,
         [flat],
-        (VMEM,) * 5, (own, from_far, from_near, codes, coef),
-        [VMEM((z.nv, width, LANES), f32), VMEM((z.nv, LANES, LANES), f32)],
+        (VMEM,) * 5, (parts, from_far, from_near, refs, own_source),
+        [VMEM((SUB, z.cols), i32), VMEM((NPTS * NPTS, LANES), f32), VMEM((z.nv, width, LANES), f32), VMEM((z.nv, LANES, LANES), f32)],
         flops=10**8, nbytes=3 * 10**6,
     )
     whole_weight = 36.0 * 4.0 * elems * count * levels * lax.axis_size("lev")

time: 23.1 us -> 23 us (level)
  starting transfers between devices: 10.9 us -> 11.3 us
  waiting for transfers between devices: 5.54 us -> 5.3 us
    ppermute x1, starting transfers between devices: 3.21 us -> 3.53 us  [per_device(): from_far = lax.ppermute(to_far, 'elem', far)]
    ppermute x1, waiting for transfers between devices: 1.06 us -> 0.83 us  [per_device(): from_far = lax.ppermute(to_far, 'elem', far)]
where the time goes in v6:
time: 23 us; the launch traced here: 22.8 us
  starting transfers between devices  11.3 us (49%)
  Pallas kernels  6.2 us (27%)
  waiting for transfers between devices  5.3 us (23%)
    pallas_call x5, Pallas kernels, call(): pl.pallas_call(functools.partial(kernel, z), out_shape=[jax.ShapeDtypeStr...  6.2 us
    ppermute x1, starting transfers between devices, per_device(): in_far = lax.ppermute(ask_far, 'elem', far)  4.58 us
    all_to_all x1, waiting for transfers between devices, per_device(): every = lax.all_to_all(spread, axes, 0, 0)  4.46 us
    ppermute x1, starting transfers between devices, per_device(): from_far = lax.ppermute(to_far, 'elem', far)  3.53 us
    all_to_all x1, starting transfers between devices, per_device(): every = lax.all_to_all(spread, axes, 0, 0)  3.14 us
    ppermute x1, waiting for transfers between devices, per_device(): from_far = lax.ppermute(to_far, 'elem', far)  0.83 us
  transfers between devices with their start and end apart: 5, of which 2 were waited for; matrix products, arithmetic and copies ran while one was open for 0% of the time, Pallas kernels for 15%

profile of v6, /device:TPU:0, one launch (start us, length us, event | category | flops | bytes accessed | tf_op | source)
XLA Modules:
  0.0 22.8 jit_solution(11535319269035001166)
XLA Ops:
  0.0 0.0 copy-start
  0.0 1.1 %shard_map.55 = (f32[32,128]{1,0:T(8,128)S(1)}, f32[40,128]{1,0:T(8,128)S(1)}, f32[40,128]{1,0:T(8,128)S(1)}, s32[16,64]{1,0:T(8,128)S(1)}, s32[1,64]{1,0:T(1,128)S(1)}) custom-call(s32[1,2,16]{2,1,0:T(2,128)} %req_hbm.1, s32[16,64]{1,0:T(8,128)} %bitcast.4, s32[1,64]{1,0:T(1,128)} %bitcast.5), custom_call_target="tpu_custom_call" | custom-call | flops 1000000000 | bytes 10000000 | tf_op jit(solution)/shard_map/pallas_call | solution.py:308
  1.1 4.6 %collective-permute-start = (f32[40,128]{1,0:T(8,128)S(1)}, f32[40,128]{1,0:T(8,128)S(1)}, u32[]{:S(2)}, u32[]{:S(2)}) collective-permute-start(f32[40,128]{1,0:T(8,128)S(1)} %get-tuple-element.16), channel_id=1, source_target_pairs={{0,28},{4,8},{8,4},{12,16},{16,12},{20,24},{24,20},{28,0},{1,29},{... | collective-permute-start | bytes 61448 | tf_op jit(solution)/shard_map/ppermute | solution.py:338
  5.7 0.0 collective-permute-start.1
  5.7 0.0 copy-done
  5.7 1.5 %shard_map.56 = (bf16[3,640,256]{2,1,0:T(8,128)(2,1)S(1)}, f32[1280,128]{1,0:T(8,128)S(1)}) custom-call(f32[64,4,640]{2,1,0:T(4,128)S(1)} %copy-done), custom_call_target="tpu_custom_call" | custom-call | flops 100000000 | bytes 4000000 | tf_op jit(solution)/shard_map/pallas_call | solution.py:308
  7.2 0.0 collective-permute-done.infar_ref
  7.2 0.0 collective-permute-done.1.innear_ref
  7.3 0.8 %shard_map.57 = (f32[32,1,40]{2,1,0:T(1,128)}, f32[320,128]{1,0:T(8,128)S(1)}, f32[320,128]{1,0:T(8,128)S(1)}) custom-call(f32[32,128]{1,0:T(8,128)S(1)} %get-tuple-element.15.wown_ref, f32[40,128]{1,0:T(8,128)S(1)} %collective-permute-done.infar_ref, f32[40,128]{1,0:T(8,128)S(1)} %collective-permute-done.1.innear_ref, ...), custom_call_target="tpu_custom_call" | custom-call | flops 10000000 | bytes 3000000 | tf_op jit(solution)/shard_map/pallas_call | solution.py:308
  8.0 3.5 %collective-permute-start.2 = (f32[320,128]{1,0:T(8,128)S(1)}, f32[320,128]{1,0:T(8,128)S(1)}, u32[]{:S(2)}, u32[]{:S(2)}) collective-permute-start(f32[320,128]{1,0:T(8,128)S(1)} %get-tuple-element.21), channel_id=1, source_target_pairs={{0,28},{4,8},{8,4},{12,16},{16,12},{20,24},{24,20},{28,0},{1,29},{... | collective-permute-start | bytes 491528 | tf_op jit(solution)/shard_map/ppermute | solution.py:354
  11.6 0.0 collective-permute-start.3
  11.6 3.1 %all-to-all-start = ((f32[32,1,40]{2,1,0:T(1,128)}), f32[32,1,40]{2,1,0:T(1,128)S(1)}, u32[]{:S(2)}, u32[]{:S(2)}) async-start(f32[32,1,40]{2,1,0:T(1,128)} %get-tuple-element.20), calls=%async_computation | async-start | bytes 32768 | tf_op jit(solution)/shard_map/all_to_all | solution.py:356
  14.7 0.8 %collective-permute-done.2.far_ref = f32[320,128]{1,0:T(8,128)S(1)} collective-permute-done((f32[320,128]{1,0:T(8,128)S(1)}, f32[320,128]{1,0:T(8,128)S(1)}, u32[]{:S(2)}, u32[]{:S(2)}) %collective-permute-start.2) | collective-permute-done | bytes 163872 | tf_op jit(solution)/shard_map/ppermute | solution.py:354
  15.6 0.0 collective-permute-done.3.near_ref
  15.6 1.8 %shard_map.58.refs_2_ = f32[5,256,128]{2,1,0:T(8,128)S(1)} custom-call(bf16[3,640,256]{2,1,0:T(8,128)(2,1)S(1)} %get-tuple-element.19.parts_ref, f32[320,128]{1,0:T(8,128)S(1)} %collective-permute-done.2.far_ref, f32[320,128]{1,0:T(8,128)S(1)} %collective-permute-done.3.near_ref, s32[16,64]{1,0:T(8,128)S(1)} %get-tuple-element.23.ref_ref, ...), custom_call_target="tpu_custom_call" | custom-call | flops 100000000 | bytes 3000000 | tf_op jit(solution)/shard_map/pallas_call | solution.py:308
  17.4 0.0 copy-start.1
  17.4 4.5 %all-to-all-done.refs_0_ = f32[32,1,40]{2,1,0:T(1,128)S(1)} async-done(((f32[32,1,40]{2,1,0:T(1,128)}), f32[32,1,40]{2,1,0:T(1,128)S(1)}, u32[]{:S(2)}, u32[]{:S(2)}) %all-to-all-start) | async-done | bytes 5152 | tf_op jit(solution)/shard_map/all_to_all | solution.py:356
  21.9 0.0 copy-done.1
  21.9 1.0 %shard_map.59 = f32[64,4,640]{2,1,0:T(4,128)} custom-call(f32[32,1,40]{2,1,0:T(1,128)S(1)} %all-to-all-done.refs_0_, f32[1,40]{1,0:T(1,128)S(1)} %bitcast.3, f32[5,256,128]{2,1,0:T(8,128)S(1)} %shard_map.58.refs_2_), custom_call_target="tpu_custom_call" | custom-call | flops 1000000 | bytes 1000000 | tf_op jit(solution)/shard_map/pallas_call | solution.py:308
Async XLA Ops:
  0.0 5.7 %copy-start = (f32[64,4,640]{2,1,0:T(4,128)S(1)}, f32[64,4,640]{2,1,0:T(4,128)}, u32[]{:S(2)}) copy-start(f32[64,4,640]{2,1,0:T(4,128)} %x_ref.1) | copy-start | bytes 1966084
  1.1 6.1 %collective-permute-start = (f32[40,128]{1,0:T(8,128)S(1)}, f32[40,128]{1,0:T(8,128)S(1)}, u32[]{:S(2)}, u32[]{:S(2)}) collective-permute-start(f32[40,128]{1,0:T(8,128)S(1)} %get-tuple-element.16), channel_id=1, source_target_pairs={{0,28},{4,8},{8,4},{12,16},{16,12},{20,24},{24,20},{28,0},{1,29},{... | collective-permute-start | bytes 61448 | tf_op jit(solution)/shard_map/ppermute | solution.py:338
  5.7 1.5 %collective-permute-start.1 = (f32[40,128]{1,0:T(8,128)S(1)}, f32[40,128]{1,0:T(8,128)S(1)}, u32[]{:S(2)}, u32[]{:S(2)}) collective-permute-start(f32[40,128]{1,0:T(8,128)S(1)} %get-tuple-element.17), channel_id=1, source_target_pairs={{0,4},{4,0},{8,12},{12,8},{16,20},{20,16},{24,28},{28,24},{1,5},{5... | collective-permute-start | bytes 61448 | tf_op jit(solution)/shard_map/ppermute | solution.py:339
  8.0 7.5 %collective-permute-start.2 = (f32[320,128]{1,0:T(8,128)S(1)}, f32[320,128]{1,0:T(8,128)S(1)}, u32[]{:S(2)}, u32[]{:S(2)}) collective-permute-start(f32[320,128]{1,0:T(8,128)S(1)} %get-tuple-element.21), channel_id=1, source_target_pairs={{0,28},{4,8},{8,4},{12,16},{16,12},{20,24},{24,20},{28,0},{1,29},{... | collective-permute-start | bytes 491528 | tf_op jit(solution)/shard_map/ppermute | solution.py:354
  11.6 4.0 %collective-permute-start.3 = (f32[320,128]{1,0:T(8,128)S(1)}, f32[320,128]{1,0:T(8,128)S(1)}, u32[]{:S(2)}, u32[]{:S(2)}) collective-permute-start(f32[320,128]{1,0:T(8,128)S(1)} %get-tuple-element.22), channel_id=1, source_target_pairs={{0,4},{4,0},{8,12},{12,8},{16,20},{20,16},{24,28},{28,24},{1,5},{5... | collective-permute-start | bytes 491528 | tf_op jit(solution)/shard_map/ppermute | solution.py:355
  11.6 10.3 %all-to-all-start = ((f32[32,1,40]{2,1,0:T(1,128)}), f32[32,1,40]{2,1,0:T(1,128)S(1)}, u32[]{:S(2)}, u32[]{:S(2)}) async-start(f32[32,1,40]{2,1,0:T(1,128)} %get-tuple-element.20), calls=%async_computation | async-start | bytes 32768 | tf_op jit(solution)/shard_map/all_to_all | solution.py:356
  17.4 4.5 %copy-start.1 = (f32[40]{0:T(128)S(1)}, f32[40]{0:T(128)}, u32[]{:S(2)}) copy-start(f32[40]{0:T(128)} %param.9) | copy-start | bytes 484

commit v7 on v6

--- a/solution.py
+++ b/solution.py
@@ -69,7 +69,7 @@
 
 
 def plan_kernel(
-    z, req_hbm, ref_hbm, src_hbm, wown_ref, far_ref, near_ref, ref_ref, src_ref, req_ref, sem
+    z, req_hbm, ref_hbm, src_hbm, far_ref, note_ref, ref_ref, src_ref, req_ref, sem
 ):
     elems, slots = z.elems, z.slots
     copies = [
@@ -80,15 +80,10 @@
         copy.start()
     odd = lax.rem(lax.axis_index("elem"), 2)
     lane = lax.broadcasted_iota(jnp.int32, (1, LANES), 1)
-    group = lane // elems
-    row = lax.broadcasted_iota(jnp.int32, (z.wrows, LANES), 0) + z.wrows * group
-    srow = lax.broadcasted_iota(jnp.int32, (LANES, LANES), 0)
     k_lane = lane % slots
     for copy in copies:
         copy.wait()
-    ref = jnp.concatenate([ref_ref[...]] * z.per, axis=1)
-    counts = tree(jnp.add, [jnp.where(row == ref[p : p + 1, :], float(WEIGHT36[p]), 0.0) for p in range(NPTS)])
-    counts = counts.astype(jnp.bfloat16)
+    counts = count_points(z, ref_ref[...])
     src = jnp.concatenate([src_ref[...]] * z.per, axis=1)
     far_base, near_base = elems + odd * slots, elems + (1 - odd) * slots
     far = jnp.full((1, LANES), -1, jnp.int32)
@@ -101,17 +96,34 @@
         near = jnp.where(src == near_base + k, near_k, near)
         pat_far = jnp.where(k_lane == k, far_k, pat_far)
         pat_near = jnp.where(k_lane == k, near_k, pat_near)
-    own = jnp.where(src < elems, src, -1)
-
-    def weights(which):
-        pick = srow == jnp.where(which >= 0, which + elems * group, -1)
-        return mm_nt(counts, pick.astype(jnp.float32).astype(jnp.bfloat16))
-
-    far_ref[0 : z.wrows, :] = weights(far)
+    far_ref[0 : z.wrows, :] = weights(z, counts, far)
     far_ref[z.wrows :, :] = jnp.broadcast_to(pat_far.astype(jnp.float32), (SUB, LANES))
-    near_ref[0 : z.wrows, :] = weights(near)
-    near_ref[z.wrows :, :] = jnp.broadcast_to(pat_near.astype(jnp.float32), (SUB, LANES))
-    wown_ref[...] = weights(own)
+    note_ref[0:1, :] = near
+    note_ref[1:2, :] = pat_near
+
+
+def weights(z, counts, which):
+    lane = lax.broadcasted_iota(jnp.int32, (1, LANES), 1)
+    srow = lax.broadcasted_iota(jnp.int32, (LANES, LANES), 0)
+    pick = srow == jnp.where(which >= 0, which + z.elems * (lane // z.elems), -1)
+    return mm_nt(counts, pick.astype(jnp.float32).astype(jnp.bfloat16))
+
+
+def count_points(z, ref):
+    lane = lax.broadcasted_iota(jnp.int32, (1, LANES), 1)
+    row = lax.broadcasted_iota(jnp.int32, (z.wrows, LANES), 0) + z.wrows * (lane // z.elems)
+    ref = jnp.concatenate([ref] * z.per, axis=1)
+    return tree(
+        jnp.add, [jnp.where(row == ref[p : p + 1, :], float(WEIGHT36[p]), 0.0) for p in range(NPTS)]
+    ).astype(jnp.bfloat16)
+
+
+def beside_kernel(z, ref_ref, src_ref, note_ref, wown_ref, near_ref):
+    counts = count_points(z, ref_ref[...])
+    src = jnp.concatenate([src_ref[...]] * z.per, axis=1)
+    near_ref[0 : z.wrows, :] = weights(z, counts, note_ref[0:1, :])
+    near_ref[z.wrows :, :] = jnp.broadcast_to(note_ref[1:2, :].astype(jnp.float32), (SUB, LANES))
+    wown_ref[...] = weights(z, counts, jnp.where(src < z.elems, src, -1))
 
 
 def tables(z, src, ref, codes_ref, coef_ref):
@@ -323,19 +335,23 @@
     assert z.halves * levels * z.slots == LANES and z.part * z.halves == width
     f32, bf16, i32 = jnp.float32, jnp.bfloat16, jnp.int32
     flat = ((z.tiles, elems * levels, LANES), f32)
-    wown, ask_far, ask_near, refs, own_source = call(
+    far_ask, note, refs, own_source = call(
         plan_kernel, z,
-        [((z.wrows, LANES), f32), ((z.wrows + SUB, LANES), f32), ((z.wrows + SUB, LANES), f32),
-         ((NPTS, elems), i32), ((1, elems), i32)],
+        [((z.wrows + SUB, LANES), f32), ((SUB, LANES), i32), ((NPTS, elems), i32), ((1, elems), i32)],
         (pltpu.HBM,) * 3, [in_hbm(a) for a in (requests, ref_index.T, source.reshape(1, elems))],
         [SMEM(requests.shape, i32), pltpu.SemaphoreType.DMA((3,))],
         flops=10**9, nbytes=10**7,
+    )
+    wown, ask_near = call(
+        beside_kernel, z,
+        [((z.wrows, LANES), f32), ((z.wrows + SUB, LANES), f32)],
+        (VMEM,) * 3, (refs, own_source, note), flops=10**6, nbytes=10**5,
     )
     count = lax.axis_size("elem")
     assert count % 2 == 0
     far = [(i, (i - 1 if i % 2 == 0 else i + 1) % count) for i in range(count)]
     near = [(i, i + 1 if i % 2 == 0 else i - 1) for i in range(count)]
-    in_far = lax.ppermute(ask_far, "elem", far)
+    in_far = lax.ppermute(far_ask, "elem", far)
     in_near = lax.ppermute(ask_near, "elem", near)
     parts, sums = call(
         prep_kernel, z,

time: 23 us -> 23 us (level)
  starting transfers between devices: 11.3 us -> 11 us
    pallas_call x5 -> x6, Pallas kernels: 6.2 us -> 6.38 us  [call(): pl.pallas_call(functools.partial(kernel, z), out_shape=[jax.ShapeDtypeStr...]
  transfers between devices with their start and end apart: 5 -> 5, of which waited for: 2 -> 2; matrix products, arithmetic and copies ran while one was open for 0% -> 0% of each run, Pallas kernels for 15% -> 16%
where the time goes in v7:
time: 23 us; the launch traced here: 22.8 us
  starting transfers between devices  11 us (48%)
  Pallas kernels  6.38 us (28%)
  waiting for transfers between devices  5.3 us (23%)
    pallas_call x6, Pallas kernels, call(): pl.pallas_call(functools.partial(kernel, z), out_shape=[jax.ShapeDtypeStr...  6.38 us
    ppermute x1, starting transfers between devices, per_device(): in_far = lax.ppermute(far_ask, 'elem', far)  4.58 us
    all_to_all x1, waiting for transfers between devices, per_device(): every = lax.all_to_all(spread, axes, 0, 0)  4.32 us
    ppermute x1, starting transfers between devices, per_device(): from_far = lax.ppermute(to_far, 'elem', far)  3.3 us
    all_to_all x1, starting transfers between devices, per_device(): every = lax.all_to_all(spread, axes, 0, 0)  3.14 us
    ppermute x1, waiting for transfers between devices, per_device(): from_far = lax.ppermute(to_far, 'elem', far)  0.97 us
  transfers between devices with their start and end apart: 5, of which 2 were waited for; matrix products, arithmetic and copies ran while one was open for 0% of the time, Pallas kernels for 16%

profile of v7, /device:TPU:0, one launch (start us, length us, event | category | flops | bytes accessed | tf_op | source)
XLA Modules:
  0.0 22.8 jit_solution(10272169668827020397)
XLA Ops:
  0.0 0.0 copy-start
  0.0 1.1 %shard_map.55 = (f32[40,128]{1,0:T(8,128)S(1)}, s32[8,128]{1,0:T(8,128)S(1)}, s32[16,64]{1,0:T(8,128)S(1)}, s32[1,64]{1,0:T(1,128)S(1)}) custom-call(s32[1,2,16]{2,1,0:T(2,128)} %req_hbm.1, s32[16,64]{1,0:T(8,128)} %bitcast.4, s32[1,64]{1,0:T(1,128)} %bitcast.5), custom_call_target="tpu_custom_call" | custom-call | flops 1000000000 | bytes 10000000 | tf_op jit(solution)/shard_map/pallas_call | solution.py:320
  1.1 4.6 %collective-permute-start = (f32[40,128]{1,0:T(8,128)S(1)}, f32[40,128]{1,0:T(8,128)S(1)}, u32[]{:S(2)}, u32[]{:S(2)}) collective-permute-start(f32[40,128]{1,0:T(8,128)S(1)} %get-tuple-element.20), channel_id=1, source_target_pairs={{0,28},{4,8},{8,4},{12,16},{16,12},{20,24},{24,20},{28,0},{1,29},{... | collective-permute-start | bytes 61448 | tf_op jit(solution)/shard_map/ppermute | solution.py:354
  5.7 0.2 shard_map.56
  5.9 0.0 collective-permute-start.1
  5.9 0.0 copy-done
  5.9 1.5 %shard_map.57 = (bf16[3,640,256]{2,1,0:T(8,128)(2,1)S(1)}, f32[1280,128]{1,0:T(8,128)S(1)}) custom-call(f32[64,4,640]{2,1,0:T(4,128)S(1)} %copy-done), custom_call_target="tpu_custom_call" | custom-call | flops 100000000 | bytes 4000000 | tf_op jit(solution)/shard_map/pallas_call | solution.py:320
  7.4 0.0 collective-permute-done.infar_ref
  7.4 0.0 collective-permute-done.1.innear_ref
  7.4 0.8 %shard_map.58 = (f32[32,1,40]{2,1,0:T(1,128)}, f32[320,128]{1,0:T(8,128)S(1)}, f32[320,128]{1,0:T(8,128)S(1)}) custom-call(f32[32,128]{1,0:T(8,128)S(1)} %get-tuple-element.19.wown_ref, f32[40,128]{1,0:T(8,128)S(1)} %collective-permute-done.infar_ref, f32[40,128]{1,0:T(8,128)S(1)} %collective-permute-done.1.innear_ref, ...), custom_call_target="tpu_custom_call" | custom-call | flops 10000000 | bytes 3000000 | tf_op jit(solution)/shard_map/pallas_call | solution.py:320
  8.2 3.3 %collective-permute-start.2 = (f32[320,128]{1,0:T(8,128)S(1)}, f32[320,128]{1,0:T(8,128)S(1)}, u32[]{:S(2)}, u32[]{:S(2)}) collective-permute-start(f32[320,128]{1,0:T(8,128)S(1)} %get-tuple-element.25), channel_id=1, source_target_pairs={{0,28},{4,8},{8,4},{12,16},{16,12},{20,24},{24,20},{28,0},{1,29},{... | collective-permute-start | bytes 491528 | tf_op jit(solution)/shard_map/ppermute | solution.py:370
  11.5 0.0 collective-permute-start.3
  11.5 3.1 %all-to-all-start = ((f32[32,1,40]{2,1,0:T(1,128)}), f32[32,1,40]{2,1,0:T(1,128)S(1)}, u32[]{:S(2)}, u32[]{:S(2)}) async-start(f32[32,1,40]{2,1,0:T(1,128)} %get-tuple-element.24), calls=%async_computation | async-start | bytes 32768 | tf_op jit(solution)/shard_map/all_to_all | solution.py:372
  14.7 1.0 %collective-permute-done.2.far_ref = f32[320,128]{1,0:T(8,128)S(1)} collective-permute-done((f32[320,128]{1,0:T(8,128)S(1)}, f32[320,128]{1,0:T(8,128)S(1)}, u32[]{:S(2)}, u32[]{:S(2)}) %collective-permute-start.2) | collective-permute-done | bytes 163872 | tf_op jit(solution)/shard_map/ppermute | solution.py:370
  15.7 0.0 collective-permute-done.3.near_ref
  15.7 1.8 %shard_map.59.refs_2_ = f32[5,256,128]{2,1,0:T(8,128)S(1)} custom-call(bf16[3,640,256]{2,1,0:T(8,128)(2,1)S(1)} %get-tuple-element.23.parts_ref, f32[320,128]{1,0:T(8,128)S(1)} %collective-permute-done.2.far_ref, f32[320,128]{1,0:T(8,128)S(1)} %collective-permute-done.3.near_ref, s32[16,64]{1,0:T(8,128)S(1)} %get-tuple-element.16.ref_ref, ...), custom_call_target="tpu_custom_call" | custom-call | flops 100000000 | bytes 3000000 | tf_op jit(solution)/shard_map/pallas_call | solution.py:320
  17.5 0.0 copy-start.1
  17.5 4.3 %all-to-all-done.refs_0_ = f32[32,1,40]{2,1,0:T(1,128)S(1)} async-done(((f32[32,1,40]{2,1,0:T(1,128)}), f32[32,1,40]{2,1,0:T(1,128)S(1)}, u32[]{:S(2)}, u32[]{:S(2)}) %all-to-all-start) | async-done | bytes 5152 | tf_op jit(solution)/shard_map/all_to_all | solution.py:372
  21.8 0.0 copy-done.1
  21.8 1.0 %shard_map.60 = f32[64,4,640]{2,1,0:T(4,128)} custom-call(f32[32,1,40]{2,1,0:T(1,128)S(1)} %all-to-all-done.refs_0_, f32[1,40]{1,0:T(1,128)S(1)} %bitcast.3, f32[5,256,128]{2,1,0:T(8,128)S(1)} %shard_map.59.refs_2_), custom_call_target="tpu_custom_call" | custom-call | flops 1000000 | bytes 1000000 | tf_op jit(solution)/shard_map/pallas_call | solution.py:320
Async XLA Ops:
  0.0 5.9 %copy-start = (f32[64,4,640]{2,1,0:T(4,128)S(1)}, f32[64,4,640]{2,1,0:T(4,128)}, u32[]{:S(2)}) copy-start(f32[64,4,640]{2,1,0:T(4,128)} %x_ref.1) | copy-start | bytes 1966084
  1.1 6.3 %collective-permute-start = (f32[40,128]{1,0:T(8,128)S(1)}, f32[40,128]{1,0:T(8,128)S(1)}, u32[]{:S(2)}, u32[]{:S(2)}) collective-permute-start(f32[40,128]{1,0:T(8,128)S(1)} %get-tuple-element.20), channel_id=1, source_target_pairs={{0,28},{4,8},{8,4},{12,16},{16,12},{20,24},{24,20},{28,0},{1,29},{... | collective-permute-start | bytes 61448 | tf_op jit(solution)/shard_map/ppermute | solution.py:354
  5.9 1.5 %collective-permute-start.1 = (f32[40,128]{1,0:T(8,128)S(1)}, f32[40,128]{1,0:T(8,128)S(1)}, u32[]{:S(2)}, u32[]{:S(2)}) collective-permute-start(f32[40,128]{1,0:T(8,128)S(1)} %get-tuple-element.21), channel_id=1, source_target_pairs={{0,4},{4,0},{8,12},{12,8},{16,20},{20,16},{24,28},{28,24},{1,5},{5... | collective-permute-start | bytes 61448 | tf_op jit(solution)/shard_map/ppermute | solution.py:355
  8.2 7.4 %collective-permute-start.2 = (f32[320,128]{1,0:T(8,128)S(1)}, f32[320,128]{1,0:T(8,128)S(1)}, u32[]{:S(2)}, u32[]{:S(2)}) collective-permute-start(f32[320,128]{1,0:T(8,128)S(1)} %get-tuple-element.25), channel_id=1, source_target_pairs={{0,28},{4,8},{8,4},{12,16},{16,12},{20,24},{24,20},{28,0},{1,29},{... | collective-permute-start | bytes 491528 | tf_op jit(solution)/shard_map/ppermute | solution.py:370
  11.5 4.1 %collective-permute-start.3 = (f32[320,128]{1,0:T(8,128)S(1)}, f32[320,128]{1,0:T(8,128)S(1)}, u32[]{:S(2)}, u32[]{:S(2)}) collective-permute-start(f32[320,128]{1,0:T(8,128)S(1)} %get-tuple-element.26), channel_id=1, source_target_pairs={{0,4},{4,0},{8,12},{12,8},{16,20},{20,16},{24,28},{28,24},{1,5},{5... | collective-permute-start | bytes 491528 | tf_op jit(solution)/shard_map/ppermute | solution.py:371
  11.5 10.3 %all-to-all-start = ((f32[32,1,40]{2,1,0:T(1,128)}), f32[32,1,40]{2,1,0:T(1,128)S(1)}, u32[]{:S(2)}, u32[]{:S(2)}) async-start(f32[32,1,40]{2,1,0:T(1,128)} %get-tuple-element.24), calls=%async_computation | async-start | bytes 32768 | tf_op jit(solution)/shard_map/all_to_all | solution.py:372
  17.5 4.3 %copy-start.1 = (f32[40]{0:T(128)S(1)}, f32[40]{0:T(128)}, u32[]{:S(2)}) copy-start(f32[40]{0:T(128)} %param.9) | copy-start | bytes 484

commit v8 on v6

--- a/solution.py
+++ b/solution.py
@@ -201,12 +201,12 @@
 
 
 def serve_kernel(
-    z, wown_ref, infar_ref, innear_ref, sums_ref, parts_ref, spread_hbm, tofar_ref, tonear_ref, weight_ref, mass_ref, sem
+    z, wown_ref, infar_ref, innear_ref, sums_ref, parts_ref, spread_hbm, tofar_ref, tonear_ref, mass_ref, sem
 ):
-    weight_ref[...] = wown_ref[...] + infar_ref[0 : z.wrows, :] + innear_ref[0 : z.wrows, :]
+    weight = wown_ref[...] + infar_ref[0 : z.wrows, :] + innear_ref[0 : z.wrows, :]
     terms = [[] for _ in range(z.tiles)]
     for r in range(z.wrows):
-        w = weight_ref[pl.ds(r, 1), :]
+        w = weight[r : r + 1, :]
         for j in range(z.tiles):
             lo = r * z.tracers + j * z.tpt
             term = sums_ref[lo : lo + z.tpt, :] * w
@@ -348,7 +348,7 @@
         serve_kernel, z,
         [spread_shape, ((z.part, LANES), f32), ((z.part, LANES), f32)],
         (VMEM,) * 5, (wown, in_far, in_near, sums, parts),
-        [VMEM((z.wrows, LANES), f32), VMEM(*spread_shape), pltpu.SemaphoreType.DMA(())],
+        [VMEM(*spread_shape), pltpu.SemaphoreType.DMA(())],
         flops=10**7, nbytes=3 * 10**6, spaces=(pltpu.HBM, VMEM, VMEM),
     )
     from_far = lax.ppermute(to_far, "elem", far)

time: 23 us -> 23 us (level)
  no operation moved by 1% of the time
where the time goes in v8:
time: 23 us; the launch traced here: 22.8 us
  starting transfers between devices  11.3 us (49%)
  Pallas kernels  6.2 us (27%)
  waiting for transfers between devices  5.3 us (23%)
    pallas_call x5, Pallas kernels, call(): pl.pallas_call(functools.partial(kernel, z), out_shape=[jax.ShapeDtypeStr...  6.2 us
    ppermute x1, starting transfers between devices, per_device(): in_far = lax.ppermute(ask_far, 'elem', far)  4.58 us
    all_to_all x1, waiting for transfers between devices, per_device(): every = lax.all_to_all(spread, axes, 0, 0)  4.46 us
    ppermute x1, starting transfers between devices, per_device(): from_far = lax.ppermute(to_far, 'elem', far)  3.53 us
    all_to_all x1, starting transfers between devices, per_device(): every = lax.all_to_all(spread, axes, 0, 0)  3.14 us
    ppermute x1, waiting for transfers between devices, per_device(): from_far = lax.ppermute(to_far, 'elem', far)  0.83 us
  transfers between devices with their start and end apart: 5, of which 2 were waited for; matrix products, arithmetic and copies ran while one was open for 0% of the time, Pallas kernels for 15%

profile of v8, /device:TPU:0, one launch (start us, length us, event | category | flops | bytes accessed | tf_op | source)
XLA Modules:
  0.0 22.8 jit_solution(10974395739778017858)
XLA Ops:
  0.0 0.0 copy-start
  0.0 1.1 %shard_map.55 = (f32[32,128]{1,0:T(8,128)S(1)}, f32[40,128]{1,0:T(8,128)S(1)}, f32[40,128]{1,0:T(8,128)S(1)}, s32[16,64]{1,0:T(8,128)S(1)}, s32[1,64]{1,0:T(1,128)S(1)}) custom-call(s32[1,2,16]{2,1,0:T(2,128)} %req_hbm.1, s32[16,64]{1,0:T(8,128)} %bitcast.4, s32[1,64]{1,0:T(1,128)} %bitcast.5), custom_call_target="tpu_custom_call" | custom-call | flops 1000000000 | bytes 10000000 | tf_op jit(solution)/shard_map/pallas_call | solution.py:308
  1.1 4.6 %collective-permute-start = (f32[40,128]{1,0:T(8,128)S(1)}, f32[40,128]{1,0:T(8,128)S(1)}, u32[]{:S(2)}, u32[]{:S(2)}) collective-permute-start(f32[40,128]{1,0:T(8,128)S(1)} %get-tuple-element.16), channel_id=1, source_target_pairs={{0,28},{4,8},{8,4},{12,16},{16,12},{20,24},{24,20},{28,0},{1,29},{... | collective-permute-start | bytes 61448 | tf_op jit(solution)/shard_map/ppermute | solution.py:338
  5.7 0.0 collective-permute-start.1
  5.7 0.0 copy-done
  5.7 1.5 %shard_map.56 = (bf16[3,640,256]{2,1,0:T(8,128)(2,1)S(1)}, f32[1280,128]{1,0:T(8,128)S(1)}) custom-call(f32[64,4,640]{2,1,0:T(4,128)S(1)} %copy-done), custom_call_target="tpu_custom_call" | custom-call | flops 100000000 | bytes 4000000 | tf_op jit(solution)/shard_map/pallas_call | solution.py:308
  7.2 0.0 collective-permute-done.infar_ref
  7.2 0.0 collective-permute-done.1.innear_ref
  7.3 0.8 %shard_map.57 = (f32[32,1,40]{2,1,0:T(1,128)}, f32[320,128]{1,0:T(8,128)S(1)}, f32[320,128]{1,0:T(8,128)S(1)}) custom-call(f32[32,128]{1,0:T(8,128)S(1)} %get-tuple-element.15.wown_ref, f32[40,128]{1,0:T(8,128)S(1)} %collective-permute-done.infar_ref, f32[40,128]{1,0:T(8,128)S(1)} %collective-permute-done.1.innear_ref, ...), custom_call_target="tpu_custom_call" | custom-call | flops 10000000 | bytes 3000000 | tf_op jit(solution)/shard_map/pallas_call | solution.py:308
  8.0 3.5 %collective-permute-start.2 = (f32[320,128]{1,0:T(8,128)S(1)}, f32[320,128]{1,0:T(8,128)S(1)}, u32[]{:S(2)}, u32[]{:S(2)}) collective-permute-start(f32[320,128]{1,0:T(8,128)S(1)} %get-tuple-element.21), channel_id=1, source_target_pairs={{0,28},{4,8},{8,4},{12,16},{16,12},{20,24},{24,20},{28,0},{1,29},{... | collective-permute-start | bytes 491528 | tf_op jit(solution)/shard_map/ppermute | solution.py:354
  11.6 0.0 collective-permute-start.3
  11.6 3.1 %all-to-all-start = ((f32[32,1,40]{2,1,0:T(1,128)}), f32[32,1,40]{2,1,0:T(1,128)S(1)}, u32[]{:S(2)}, u32[]{:S(2)}) async-start(f32[32,1,40]{2,1,0:T(1,128)} %get-tuple-element.20), calls=%async_computation | async-start | bytes 32768 | tf_op jit(solution)/shard_map/all_to_all | solution.py:356
  14.7 0.8 %collective-permute-done.2.far_ref = f32[320,128]{1,0:T(8,128)S(1)} collective-permute-done((f32[320,128]{1,0:T(8,128)S(1)}, f32[320,128]{1,0:T(8,128)S(1)}, u32[]{:S(2)}, u32[]{:S(2)}) %collective-permute-start.2) | collective-permute-done | bytes 163872 | tf_op jit(solution)/shard_map/ppermute | solution.py:354
  15.6 0.0 collective-permute-done.3.near_ref
  15.6 1.8 %shard_map.58.refs_2_ = f32[5,256,128]{2,1,0:T(8,128)S(1)} custom-call(bf16[3,640,256]{2,1,0:T(8,128)(2,1)S(1)} %get-tuple-element.19.parts_ref, f32[320,128]{1,0:T(8,128)S(1)} %collective-permute-done.2.far_ref, f32[320,128]{1,0:T(8,128)S(1)} %collective-permute-done.3.near_ref, s32[16,64]{1,0:T(8,128)S(1)} %get-tuple-element.23.ref_ref, ...), custom_call_target="tpu_custom_call" | custom-call | flops 100000000 | bytes 3000000 | tf_op jit(solution)/shard_map/pallas_call | solution.py:308
  17.4 0.0 copy-start.1
  17.4 4.5 %all-to-all-done.refs_0_ = f32[32,1,40]{2,1,0:T(1,128)S(1)} async-done(((f32[32,1,40]{2,1,0:T(1,128)}), f32[32,1,40]{2,1,0:T(1,128)S(1)}, u32[]{:S(2)}, u32[]{:S(2)}) %all-to-all-start) | async-done | bytes 5152 | tf_op jit(solution)/shard_map/all_to_all | solution.py:356
  21.8 0.0 copy-done.1
  21.9 1.0 %shard_map.59 = f32[64,4,640]{2,1,0:T(4,128)} custom-call(f32[32,1,40]{2,1,0:T(1,128)S(1)} %all-to-all-done.refs_0_, f32[1,40]{1,0:T(1,128)S(1)} %bitcast.3, f32[5,256,128]{2,1,0:T(8,128)S(1)} %shard_map.58.refs_2_), custom_call_target="tpu_custom_call" | custom-call | flops 1000000 | bytes 1000000 | tf_op jit(solution)/shard_map/pallas_call | solution.py:308
Async XLA Ops:
  0.0 5.7 %copy-start = (f32[64,4,640]{2,1,0:T(4,128)S(1)}, f32[64,4,640]{2,1,0:T(4,128)}, u32[]{:S(2)}) copy-start(f32[64,4,640]{2,1,0:T(4,128)} %x_ref.1) | copy-start | bytes 1966084
  1.1 6.1 %collective-permute-start = (f32[40,128]{1,0:T(8,128)S(1)}, f32[40,128]{1,0:T(8,128)S(1)}, u32[]{:S(2)}, u32[]{:S(2)}) collective-permute-start(f32[40,128]{1,0:T(8,128)S(1)} %get-tuple-element.16), channel_id=1, source_target_pairs={{0,28},{4,8},{8,4},{12,16},{16,12},{20,24},{24,20},{28,0},{1,29},{... | collective-permute-start | bytes 61448 | tf_op jit(solution)/shard_map/ppermute | solution.py:338
  5.7 1.5 %collective-permute-start.1 = (f32[40,128]{1,0:T(8,128)S(1)}, f32[40,128]{1,0:T(8,128)S(1)}, u32[]{:S(2)}, u32[]{:S(2)}) collective-permute-start(f32[40,128]{1,0:T(8,128)S(1)} %get-tuple-element.17), channel_id=1, source_target_pairs={{0,4},{4,0},{8,12},{12,8},{16,20},{20,16},{24,28},{28,24},{1,5},{5... | collective-permute-start | bytes 61448 | tf_op jit(solution)/shard_map/ppermute | solution.py:339
  8.0 7.5 %collective-permute-start.2 = (f32[320,128]{1,0:T(8,128)S(1)}, f32[320,128]{1,0:T(8,128)S(1)}, u32[]{:S(2)}, u32[]{:S(2)}) collective-permute-start(f32[320,128]{1,0:T(8,128)S(1)} %get-tuple-element.21), channel_id=1, source_target_pairs={{0,28},{4,8},{8,4},{12,16},{16,12},{20,24},{24,20},{28,0},{1,29},{... | collective-permute-start | bytes 491528 | tf_op jit(solution)/shard_map/ppermute | solution.py:354
  11.6 4.0 %collective-permute-start.3 = (f32[320,128]{1,0:T(8,128)S(1)}, f32[320,128]{1,0:T(8,128)S(1)}, u32[]{:S(2)}, u32[]{:S(2)}) collective-permute-start(f32[320,128]{1,0:T(8,128)S(1)} %get-tuple-element.22), channel_id=1, source_target_pairs={{0,4},{4,0},{8,12},{12,8},{16,20},{20,16},{24,28},{28,24},{1,5},{5... | collective-permute-start | bytes 491528 | tf_op jit(solution)/shard_map/ppermute | solution.py:355
  11.6 10.3 %all-to-all-start = ((f32[32,1,40]{2,1,0:T(1,128)}), f32[32,1,40]{2,1,0:T(1,128)S(1)}, u32[]{:S(2)}, u32[]{:S(2)}) async-start(f32[32,1,40]{2,1,0:T(1,128)} %get-tuple-element.20), calls=%async_computation | async-start | bytes 32768 | tf_op jit(solution)/shard_map/all_to_all | solution.py:356
  17.4 4.5 %copy-start.1 = (f32[40]{0:T(128)S(1)}, f32[40]{0:T(128)}, u32[]{:S(2)}) copy-start(f32[40]{0:T(128)} %param.9) | copy-start | bytes 484
